TPU v7x, 512 devices: a whole 4x8x8 slice. The times are simulated.
512 devices in a mesh: energy: 16 (over z, core), rows: 32 (over y, x).
Axes of the slice: x: 4, y: 8, z: 8, core: 2. Of those that a mesh axis runs over, the one named last changes fastest.
Arguments:
- coupling: bfloat16 [2, 512, 512], replicated, may hold values from -4.1875 to 4.1875
- inverses: bfloat16 [512, 4, 2, 256, 256], P(('energy', 'rows')), may hold values from -0.0078125 to 0.0078125
- contact_row: int32 [48], replicated, may hold values from 0 to 31, as said below
- assignment: int32 [128], P('energy'), may hold values from 0 to 127, as said below
- states: bfloat16 [48, 2, 16, 512], replicated, may hold values from -0.119628906 to 0.119628906
- weights: float32 [128], P('energy'), may hold values from 0.03 to 0.3
Outputs:
- injection: float32 [128, 32, 2, 16, 512], P('energy', 'rows')
- integrated: float32 [32, 2, 16, 512], P('rows')
- far_forward: bfloat16 [512, 2, 256, 256], P(('energy', 'rows'))
- far_backward: bfloat16 [512, 2, 256, 256], P(('energy', 'rows'))
Inputs may be any that keep to these rules, and one draw needn't show every extreme that they name: `contact_row`: every device block row has one contact or more. `assignment`: each aligned block of 8 entries, b * 8 to b * 8 + 7, holds each of those same numbers once.
All inputs are finite; a program needn't handle non-finite values.
Results may differ from a plain program's by a relative error of at most 0.024.
Values may be sent and summed in bfloat16 or wider, within the bound.
No kernel may reach another device: no remote copies, remote signals or barrier semaphores. Data moves between devices by JAX's collectives and lax.ppermute only.
A program may use at most 64 MiB of HBM per device.

v0:
```python
import jax
import jax.numpy as jnp
from jax import lax
from jax.sharding import PartitionSpec as P

ITERS = 4
ROWS_DEV = 1


def partner(shard, axis, stride):
    return lax.ppermute(shard, axis, [(i, i ^ 1 << stride) for i in range(lax.axis_size(axis))])


def from_everyone(shard, axis):
    copies = jnp.broadcast_to(shard, (lax.axis_size(axis), *shard.shape))
    return lax.all_to_all(copies, axis, split_axis=0, concat_axis=0, tiled=True)


def of_everyone(shard, axis):
    everything = from_everyone(shard, axis)
    return jnp.sum(everything.astype(jnp.float32), axis=0)


def single(leading, trailing):
    return jnp.dot(leading, trailing, preferred_element_type=jnp.float32)


def paired_dot(first_left, first_right, second_left, second_right):
    real_part = (
        single(first_left[0], first_right[0])
        - single(first_left[1], first_right[1])
        + single(second_left[0], second_right[0])
        - single(second_left[1], second_right[1])
    )
    imag_part = (
        single(first_left[0], first_right[1])
        + single(first_left[1], first_right[0])
        + single(second_left[0], second_right[1])
        + single(second_left[1], second_right[0])
    )
    return jnp.stack([real_part, imag_part])


def block_product(own_left, other_left, own_right, other_right, row_bit, column_bit):

    def aligned():
        return paired_dot(own_left, own_right, other_left, other_right)

    def crossed():
        return paired_dot(own_left, other_right, other_left, own_right)

    return lax.cond(row_bit == column_bit, aligned, crossed)


def quarter(matrix, row_half, column_half, half_order):
    return lax.dynamic_slice(
        matrix,
        (jnp.int32(0), row_half * half_order, column_half * half_order),
        (2, half_order, half_order),
    )


def local(coupling, inverses, contact_row, assignment, states, weights):
    position = lax.axis_index("rows")
    row_bit = position // 2 % 2
    column_bit = position % 2
    half_order = inverses.shape[-1]
    forward = quarter(coupling, row_bit, column_bit, half_order)
    mirror = quarter(coupling, column_bit, row_bit, half_order)
    backward = jnp.stack([mirror[0].T, -mirror[1].T])
    surface_sum = jnp.zeros((2, half_order, half_order), jnp.float32)
    for iteration in range(ITERS):
        inverse = inverses[0, iteration]
        forward_far, backward_far = partner((forward, backward), "rows", 0)
        inverse_down, forward_down, backward_down = partner((inverse, forward, backward), "rows", 1)
        forward_green = block_product(
            forward, forward_far, inverse, inverse_down, row_bit, column_bit
        ).astype(jnp.bfloat16)
        backward_green = block_product(
            backward, backward_far, inverse, inverse_down, row_bit, column_bit
        ).astype(jnp.bfloat16)
        forward_green_far, backward_green_far = partner((forward_green, backward_green), "rows", 0)
        surface_sum = surface_sum + block_product(
            forward_green, forward_green_far, backward, backward_down, row_bit, column_bit
        )
        forward_next = block_product(
            forward_green, forward_green_far, forward, forward_down, row_bit, column_bit
        ).astype(jnp.bfloat16)
        backward = block_product(
            backward_green, backward_green_far, backward, backward_down, row_bit, column_bit
        ).astype(jnp.bfloat16)
        forward = forward_next
    self_energy = surface_sum.astype(jnp.bfloat16)
    groups = assignment.shape[0]
    states_count = states.shape[2]
    contacts = contact_row.shape[0]
    flat_states = states.reshape(contacts, -1)
    block_rows = ROWS_DEV * lax.axis_size("rows")
    row_ids = jnp.arange(block_rows, dtype=jnp.int32)
    selector = (contact_row[None, :] == row_ids[:, None]).astype(jnp.bfloat16)
    drive = jnp.dot(selector, flat_states, preferred_element_type=jnp.float32).astype(jnp.bfloat16)
    drive = drive.reshape(block_rows, 2, states_count, 2, half_order)
    drive_half = lax.dynamic_index_in_dim(drive, column_bit, axis=3, keepdims=False)

    def contract_own(energy_part, drive_part):
        return jnp.einsum(
            "mn,rkn->rkm", energy_part, drive_part, preferred_element_type=jnp.float32
        )

    real_part = contract_own(self_energy[0], drive_half[:, 0]) - contract_own(
        self_energy[1], drive_half[:, 1]
    )
    imag_part = contract_own(self_energy[0], drive_half[:, 1]) + contract_own(
        self_energy[1], drive_half[:, 0]
    )
    partial_terms = jnp.stack([real_part, imag_part], axis=1)
    received = lax.all_to_all(
        partial_terms[:, None].astype(jnp.bfloat16), "rows", split_axis=0, concat_axis=1, tiled=True
    ).astype(jnp.float32)
    summed = received.reshape(ROWS_DEV, groups, 2, 2, 2, states_count, half_order).sum(axis=3)
    slots = summed.transpose(1, 0, 3, 4, 2, 5).reshape(
        groups, ROWS_DEV, 2, states_count, 2 * half_order
    )
    local_slot = assignment % groups
    slot_index = jnp.arange(groups, dtype=jnp.int32)
    source_slot = jnp.sum(
        jnp.where(local_slot[None, :] == slot_index[:, None], slot_index[None, :], 0), axis=1
    )
    injection = jnp.take(slots, source_slot, axis=0)
    weighted = jnp.tensordot(weights, injection, axes=1, precision=lax.Precision.HIGHEST)
    integrated = of_everyone(weighted.astype(jnp.bfloat16), "energy").astype(jnp.float32)
    return (injection, integrated, forward[None], backward[None])


def solution(mesh):
    placed = (
        P(),
        P(("energy", "rows"), None, None, None, None),
        P(),
        P("energy"),
        P(),
        P("energy"),
    )
    return jax.shard_map(
        local,
        mesh=mesh,
        in_specs=placed,
        out_specs=(
            P("energy", "rows", None, None, None),
            P("rows", None, None, None),
            P(("energy", "rows"), None, None, None),
            P(("energy", "rows"), None, None, None),
        ),
        check_vma=False,
    )
```

profile of v0, /device:TPU:1, one launch (start us, length us, event | category | flops | bytes accessed | tf_op | source)
XLA Modules:
  0.0 271.7 jit_solution(5553284438510358187)
XLA Ops:
  1.7 5.5 %collective-permute-start.4 = (bf16[2,256,256]{2,1,0:T(8,128)(2,1)S(1)}, bf16[2,256,256]{2,1,0:T(8,128)(2,1)S(1)}, u32[]{:S(2)}, u32[]{:S(2)}) collective-permute-start(bf16[2,256,256]{2,1,0:T(8,128)(2,1)S(1)} %constant_dynamic-slice_fusion), channel_id=1, source_target_pairs={{0,2},{1,3},{2,0},{3,1},{4,6},{5,7},{6,4},{7,5},{8,10},{9,11},{10,... | collective-permute-start | bytes 786440 | tf_op jit(solution)/shard_map/ppermute | solution.py:11
  10.6 3.6 %collective-permute-start = (bf16[2,256,256]{2,1,0:T(8,128)(2,1)S(1)}, bf16[2,256,256]{2,1,0:T(8,128)(2,1)S(1)}, u32[]{:S(2)}, u32[]{:S(2)}) collective-permute-start(bf16[2,256,256]{2,1,0:T(8,128)(2,1)S(1)} %get-tuple-element.674), channel_id=1, source_target_pairs={{0,2},{1,3},{2,0},{3,1},{4,6},{5,7},{6,4},{7,5},{8,10},{9,11},{10,... | collective-permute-start | bytes 786440 | tf_op jit(solution)/shard_map/ppermute | solution.py:11
  23.6 3.8 %collective-permute-start.3 = (bf16[2,256,256]{2,1,0:T(8,128)(2,1)S(1)}, bf16[2,256,256]{2,1,0:T(8,128)(2,1)S(1)}, u32[]{:S(2)}, u32[]{:S(2)}) collective-permute-start(bf16[2,256,256]{2,1,0:T(8,128)(2,1)S(1)} %get-tuple-element.678), channel_id=1, source_target_pairs={{0,1},{1,0},{2,3},{3,2},{4,5},{5,4},{6,7},{7,6},{8,9},{9,8},{10,11... | collective-permute-start | bytes 786440 | tf_op jit(solution)/shard_map/ppermute | solution.py:11
  27.5 5.4 %collective-permute-start.2 = (bf16[2,256,256]{2,1,0:T(8,128)(2,1)S(1)}, bf16[2,256,256]{2,1,0:T(8,128)(2,1)}, u32[]{:S(2)}, u32[]{:S(2)}) collective-permute-start(bf16[2,256,256]{2,1,0:T(8,128)(2,1)S(1)} %pad_maximum_fusion.41), channel_id=1, source_target_pairs={{0,2},{1,3},{2,0},{3,1},{4,6},{5,7},{6,4},{7,5},{8,10},{9,11},{10,... | collective-permute-start | bytes 786440 | tf_op jit(solution)/shard_map/ppermute | solution.py:11
  43.3 4.9 %collective-permute-start.11 = (bf16[2,256,256]{2,1,0:T(8,128)(2,1)S(1)}, bf16[2,256,256]{2,1,0:T(8,128)(2,1)}, u32[]{:S(2)}, u32[]{:S(2)}) collective-permute-start(bf16[2,256,256]{2,1,0:T(8,128)(2,1)S(1)} %get-tuple-element.680), channel_id=1, source_target_pairs={{0,2},{1,3},{2,0},{3,1},{4,6},{5,7},{6,4},{7,5},{8,10},{9,11},{10,... | collective-permute-start | bytes 786440 | tf_op jit(solution)/shard_map/ppermute | solution.py:11
  49.3 5.2 %conditional.105 = (bf16[2,256,256]{2,1,0:T(8,128)(2,1)S(1)}) conditional(s32[]{:T(128)} %convert_element_type.221, (bf16[2,256,256]{2,1,0:T(8,128)(2,1)S(1)}, bf16[2,256,256]{2,1,0:T(8,128)(2,1)}, bf16[2,256,256]{2,1,0:T(8,128)(2,1)S(1)}, bf16[256,256]{1,0:T(8,128)(2,1)S(1)}, bf16[256,256]{1,0:T(8,128)(2,1)S(1)}) %tuple.379, ...), branch_computations={%region_11.12_spmd, %region_12.13_spmd} | conditional | flops 269090816 | bytes 6029320
  54.5 4.1 %collective-permute-start.14 = (bf16[2,256,256]{2,1,0:T(8,128)(2,1)S(1)}, bf16[2,256,256]{2,1,0:T(8,128)(2,1)S(1)}, u32[]{:S(2)}, u32[]{:S(2)}) collective-permute-start(bf16[2,256,256]{2,1,0:T(8,128)(2,1)S(1)} %get-tuple-element.683), channel_id=1, source_target_pairs={{0,1},{1,0},{2,3},{3,2},{4,5},{5,4},{6,7},{7,6},{8,9},{9,8},{10,11... | collective-permute-start | bytes 786440 | tf_op jit(solution)/shard_map/ppermute | solution.py:11
  64.4 4.5 %collective-permute-start.9 = (bf16[2,256,256]{2,1,0:T(8,128)(2,1)S(1)}, bf16[2,256,256]{2,1,0:T(8,128)(2,1)}, u32[]{:S(2)}, u32[]{:S(2)}) collective-permute-start(bf16[2,256,256]{2,1,0:T(8,128)(2,1)S(1)} %get-tuple-element.683), channel_id=1, source_target_pairs={{0,2},{1,3},{2,0},{3,1},{4,6},{5,7},{6,4},{7,5},{8,10},{9,11},{10,... | collective-permute-start | bytes 786440 | tf_op jit(solution)/shard_map/ppermute | solution.py:11
  70.6 3.4 %collective-permute-start.15 = (bf16[2,256,256]{2,1,0:T(8,128)(2,1)S(1)}, bf16[2,256,256]{2,1,0:T(8,128)(2,1)S(1)}, u32[]{:S(2)}, u32[]{:S(2)}) collective-permute-start(bf16[2,256,256]{2,1,0:T(8,128)(2,1)S(1)} %get-tuple-element.687), channel_id=1, source_target_pairs={{0,1},{1,0},{2,3},{3,2},{4,5},{5,4},{6,7},{7,6},{8,9},{9,8},{10,11... | collective-permute-start | bytes 786440 | tf_op jit(solution)/shard_map/ppermute | solution.py:11
  74.0 5.2 %conditional.107 = (bf16[2,256,256]{2,1,0:T(8,128)(2,1)S(1)}) conditional(s32[]{:T(128)} %convert_element_type.221, (bf16[2,256,256]{2,1,0:T(8,128)(2,1)S(1)}, bf16[2,256,256]{2,1,0:T(8,128)(2,1)}, bf16[2,256,256]{2,1,0:T(8,128)(2,1)S(1)}, bf16[2,256,256]{2,1,0:T(8,128)(2,1)S(1)}) %tuple.302, (bf16[2,256,256]{2,1,0:T(8,128)(2,1)S(1)}, ...), branch_computations={%region_15.16_spmd, %region_16.17_spmd} | conditional | flops 269090816 | bytes 6029320
  84.1 4.5 %collective-permute-done.15 = bf16[2,256,256]{2,1,0:T(8,128)(2,1)S(1)} collective-permute-done((bf16[2,256,256]{2,1,0:T(8,128)(2,1)S(1)}, bf16[2,256,256]{2,1,0:T(8,128)(2,1)S(1)}, u32[]{:S(2)}, u32[]{:S(2)}) %collective-permute-start.15) | collective-permute-done | bytes 262176 | tf_op jit(solution)/shard_map/ppermute | solution.py:11
  88.6 5.2 %conditional.110 = (bf16[2,256,256]{2,1,0:T(8,128)(2,1)S(1)}) conditional(s32[]{:T(128)} %convert_element_type.221, (bf16[2,256,256]{2,1,0:T(8,128)(2,1)S(1)}, bf16[2,256,256]{2,1,0:T(8,128)(2,1)}, bf16[2,256,256]{2,1,0:T(8,128)(2,1)S(1)}, bf16[2,256,256]{2,1,0:T(8,128)(2,1)S(1)}) %tuple.308, (bf16[2,256,256]{2,1,0:T(8,128)(2,1)S(1)}, ...), branch_computations={%region_21.22_spmd, %region_22.23_spmd} | conditional | flops 269090816 | bytes 6029320
  93.8 4.2 %collective-permute-start.21 = (bf16[2,256,256]{2,1,0:T(8,128)(2,1)S(1)}, bf16[2,256,256]{2,1,0:T(8,128)(2,1)}, u32[]{:S(2)}, u32[]{:S(2)}) collective-permute-start(bf16[2,256,256]{2,1,0:T(8,128)(2,1)S(1)} %get-tuple-element.688), channel_id=1, source_target_pairs={{0,1},{1,0},{2,3},{3,2},{4,5},{5,4},{6,7},{7,6},{8,9},{9,8},{10,11... | collective-permute-start | bytes 786440 | tf_op jit(solution)/shard_map/ppermute | solution.py:11
  98.0 5.4 %conditional.108 = (bf16[2,256,256]{2,1,0:T(8,128)(2,1)S(1)}) conditional(s32[]{:T(128)} %convert_element_type.221, (bf16[2,256,256]{2,1,0:T(8,128)(2,1)S(1)}, bf16[2,256,256]{2,1,0:T(8,128)(2,1)S(1)}, bf16[2,256,256]{2,1,0:T(8,128)(2,1)}, bf16[2,256,256]{2,1,0:T(8,128)(2,1)S(1)}) %tuple.304, (bf16[2,256,256]{2,1,0:T(8,128)(2,1)S(1)}, ...), branch_computations={%region_17.18_spmd, %region_18.19_spmd} | conditional | flops 269090816 | bytes 6029320
  107.7 4.5 %collective-permute-start.16 = (bf16[2,256,256]{2,1,0:T(8,128)(2,1)S(1)}, bf16[2,256,256]{2,1,0:T(8,128)(2,1)}, u32[]{:S(2)}, u32[]{:S(2)}) collective-permute-start(bf16[2,256,256]{2,1,0:T(8,128)(2,1)S(1)} %get-tuple-element.688), channel_id=1, source_target_pairs={{0,2},{1,3},{2,0},{3,1},{4,6},{5,7},{6,4},{7,5},{8,10},{9,11},{10,... | collective-permute-start | bytes 786440 | tf_op jit(solution)/shard_map/ppermute | solution.py:11
  112.2 5.9 %conditional.114 = (bf16[2,256,256]{2,1,0:T(8,128)(2,1)}) conditional(s32[]{:T(128)} %convert_element_type.221, (bf16[2,256,256]{2,1,0:T(8,128)(2,1)S(1)}, bf16[2,256,256]{2,1,0:T(8,128)(2,1)S(1)}, bf16[2,256,256]{2,1,0:T(8,128)(2,1)}, bf16[2,256,256]{2,1,0:T(8,128)(2,1)S(1)}) %tuple.316, (bf16[2,256,256]{2,1,0:T(8,128)(2,1)S(1)}, ...), branch_computations={%region_29.30_spmd, %region_30.31_spmd} | conditional | flops 269090816 | bytes 6029320
  121.5 5.5 %conditional.112 = (bf16[2,256,256]{2,1,0:T(8,128)(2,1)S(1)}) conditional(s32[]{:T(128)} %convert_element_type.221, (bf16[2,256,256]{2,1,0:T(8,128)(2,1)S(1)}, bf16[2,256,256]{2,1,0:T(8,128)(2,1)}, bf16[2,256,256]{2,1,0:T(8,128)(2,1)}, bf16[2,256,256]{2,1,0:T(8,128)(2,1)S(1)}) %tuple.312, (bf16[2,256,256]{2,1,0:T(8,128)(2,1)S(1)}, ...), branch_computations={%region_25.26_spmd, %region_26.27_spmd} | conditional | flops 269090816 | bytes 6029320
  126.9 5.3 %collective-permute-start.20 = (bf16[2,256,256]{2,1,0:T(8,128)(2,1)S(1)}, bf16[2,256,256]{2,1,0:T(8,128)(2,1)}, u32[]{:S(2)}, u32[]{:S(2)}) collective-permute-start(bf16[2,256,256]{2,1,0:T(8,128)(2,1)S(1)} %get-tuple-element.690), channel_id=1, source_target_pairs={{0,1},{1,0},{2,3},{3,2},{4,5},{5,4},{6,7},{7,6},{8,9},{9,8},{10,11... | collective-permute-start | bytes 786440 | tf_op jit(solution)/shard_map/ppermute | solution.py:11
  132.2 3.5 %copy.34 = bf16[6,8,32,512]{3,1,2,0:T(8,128)(2,1)} copy(bf16[6,8,32,512]{3,2,1,0:T(8,128)(2,1)} %bitcast.1815) | data formatting | bytes 3145728
  135.7 8.8 %conditional.115 = (bf16[2,256,256]{2,1,0:T(8,128)(2,1)S(1)}) conditional(s32[]{:T(128)} %convert_element_type.221, (bf16[2,256,256]{2,1,0:T(8,128)(2,1)}, bf16[2,256,256]{2,1,0:T(8,128)(2,1)}, bf16[2,256,256]{2,1,0:T(8,128)(2,1)S(1)}, bf16[2,256,256]{2,1,0:T(8,128)(2,1)S(1)}) %tuple.318, (bf16[2,256,256]{2,1,0:T(8,128)(2,1)}, ...), branch_computations={%region_31.32_spmd, %region_32.33_spmd} | conditional | flops 269090816 | bytes 6029320
  146.5 5.2 %conditional.113 = (bf16[2,256,256]{2,1,0:T(8,128)(2,1)S(1)}) conditional(s32[]{:T(128)} %convert_element_type.221, (bf16[2,256,256]{2,1,0:T(8,128)(2,1)S(1)}, bf16[2,256,256]{2,1,0:T(8,128)(2,1)S(1)}, bf16[2,256,256]{2,1,0:T(8,128)(2,1)}, bf16[2,256,256]{2,1,0:T(8,128)(2,1)S(1)}) %tuple.314, (bf16[2,256,256]{2,1,0:T(8,128)(2,1)S(1)}, ...), branch_computations={%region_27.28_spmd, %region_28.29_spmd} | conditional | flops 269090816 | bytes 6029320
  151.7 3.4 %collective-permute-start.24 = (bf16[2,256,256]{2,1,0:T(8,128)(2,1)S(1)}, bf16[2,256,256]{2,1,0:T(8,128)(2,1)}, u32[]{:S(2)}, u32[]{:S(2)}) collective-permute-start(bf16[2,256,256]{2,1,0:T(8,128)(2,1)S(1)} %get-tuple-element.691), channel_id=1, source_target_pairs={{0,1},{1,0},{2,3},{3,2},{4,5},{5,4},{6,7},{7,6},{8,9},{9,8},{10,11... | collective-permute-start | bytes 786440 | tf_op jit(solution)/shard_map/ppermute | solution.py:11
  163.9 5.2 %conditional.101 = (f32[2,256,256]{2,1,0:T(8,128)S(1)}) conditional(s32[]{:T(128)} %convert_element_type.221, (bf16[2,256,256]{2,1,0:T(8,128)(2,1)S(1)}, bf16[2,256,256]{2,1,0:T(8,128)(2,1)}, bf16[2,256,256]{2,1,0:T(8,128)(2,1)S(1)}, bf16[256,256]{1,0:T(8,128)(2,1)S(1)}, bf16[256,256]{1,0:T(8,128)(2,1)S(1)}) %tuple.381, ...), branch_computations={%region_3.4_spmd, %region_4.5_spmd} | conditional | flops 268959744 | bytes 6815752 | solution.py:52
  169.1 5.2 %conditional.106 = (f32[2,256,256]{2,1,0:T(8,128)S(1)}) conditional(s32[]{:T(128)} %convert_element_type.221, (bf16[2,256,256]{2,1,0:T(8,128)(2,1)S(1)}, bf16[2,256,256]{2,1,0:T(8,128)(2,1)}, bf16[2,256,256]{2,1,0:T(8,128)(2,1)S(1)}, bf16[2,256,256]{2,1,0:T(8,128)(2,1)S(1)}) %tuple.300, (bf16[2,256,256]{2,1,0:T(8,128)(2,1)S(1)}, ...), branch_computations={%region_13.14_spmd, %region_14.15_spmd} | conditional | flops 268959744 | bytes 6815752 | solution.py:52
  174.3 5.7 %conditional.111 = (f32[2,256,256]{2,1,0:T(8,128)S(1)}) conditional(s32[]{:T(128)} %convert_element_type.221, (bf16[2,256,256]{2,1,0:T(8,128)(2,1)S(1)}, bf16[2,256,256]{2,1,0:T(8,128)(2,1)}, bf16[2,256,256]{2,1,0:T(8,128)(2,1)}, bf16[2,256,256]{2,1,0:T(8,128)(2,1)S(1)}) %tuple.310, (bf16[2,256,256]{2,1,0:T(8,128)(2,1)S(1)}, ...), branch_computations={%region_23.24_spmd, %region_24.25_spmd} | conditional | flops 268959744 | bytes 6815752 | solution.py:52
  180.8 6.2 %conditional.116 = (f32[2,256,256]{2,1,0:T(8,128)}) conditional(s32[]{:T(128)} %convert_element_type.221, (bf16[2,256,256]{2,1,0:T(8,128)(2,1)S(1)}, bf16[2,256,256]{2,1,0:T(8,128)(2,1)}, bf16[2,256,256]{2,1,0:T(8,128)(2,1)}, bf16[2,256,256]{2,1,0:T(8,128)(2,1)S(1)}) %tuple.320, (bf16[2,256,256]{2,1,0:T(8,128)(2,1)S(1)}, ...), branch_computations={%region_33.34_spmd, %region_34.35_spmd} | conditional | flops 268959744 | bytes 6815752 | solution.py:52
  190.5 16.5 %all-to-all-start = ((bf16[32,1,2,16,256]{4,3,2,1,0:T(8,128)(2,1)}), bf16[32,1,2,16,256]{4,3,2,1,0:T(8,128)(2,1)S(1)}, u32[]{:S(2)}, u32[]{:S(2)}) async-start(bf16[32,1,2,16,256]{4,3,2,1,0:T(8,128)(2,1)} %copy.23), calls=%async_computation | async-start | bytes 1048576 | tf_op jit(solution)/shard_map/all_to_all | solution.py:117
  207.2 12.5 %all-to-all-done = bf16[32,1,2,16,256]{4,3,2,1,0:T(8,128)(2,1)S(1)} async-done(((bf16[32,1,2,16,256]{4,3,2,1,0:T(8,128)(2,1)}), bf16[32,1,2,16,256]{4,3,2,1,0:T(8,128)(2,1)S(1)}, u32[]{:S(2)}, u32[]{:S(2)}) %all-to-all-start) | async-done | bytes 524320 | tf_op jit(solution)/shard_map/all_to_all | solution.py:117
  223.2 19.4 %all-to-all-start.1 = ((bf16[16,1,2,16,512]{4,3,2,1,0:T(8,128)(2,1)}), bf16[16,1,2,16,512]{4,3,2,1,0:T(8,128)(2,1)S(1)}, u32[]{:S(2)}, u32[]{:S(2)}) async-start(bf16[16,1,2,16,512]{4,3,2,1,0:T(8,128)(2,1)} %broadcast_in_dim.47), calls=%async_computation.1 | async-start | bytes 1048576 | tf_op jit(solution)/shard_map/all_to_all | solution.py:16
  244.7 4.3 %collective-permute-start.25 = (bf16[2,256,256]{2,1,0:T(8,128)(2,1)S(1)}, bf16[2,256,256]{2,1,0:T(8,128)(2,1)S(1)}, u32[]{:S(2)}, u32[]{:S(2)}) collective-permute-start(bf16[2,256,256]{2,1,0:T(8,128)(2,1)S(1)} %get-tuple-element.690), channel_id=1, source_target_pairs={{0,2},{1,3},{2,0},{3,1},{4,6},{5,7},{6,4},{7,5},{8,10},{9,11},{10,... | collective-permute-start | bytes 786440 | tf_op jit(solution)/shard_map/ppermute | solution.py:11
  259.0 5.2 %conditional.117 = (bf16[1,2,256,256]{3,2,1,0:T(8,128)(2,1)S(1)}) conditional(s32[]{:T(128)} %convert_element_type.221, (bf16[2,256,256]{2,1,0:T(8,128)(2,1)S(1)}, bf16[2,256,256]{2,1,0:T(8,128)(2,1)S(1)}, bf16[2,256,256]{2,1,0:T(8,128)(2,1)}, bf16[2,256,256]{2,1,0:T(8,128)(2,1)S(1)}) %tuple.322, (bf16[2,256,256]{2,1,0:T(8,128)(2,1)S(1)}, ...), branch_computations={%region_37.38_spmd, %region_38.39_spmd} | conditional | flops 269090816 | bytes 6029320
  264.9 5.2 %conditional.119 = (bf16[1,2,256,256]{3,2,1,0:T(8,128)(2,1)S(1)}) conditional(s32[]{:T(128)} %convert_element_type.221, (bf16[2,256,256]{2,1,0:T(8,128)(2,1)S(1)}, bf16[2,256,256]{2,1,0:T(8,128)(2,1)}, bf16[2,256,256]{2,1,0:T(8,128)(2,1)S(1)}, bf16[2,256,256]{2,1,0:T(8,128)(2,1)S(1)}) %tuple.326, (bf16[2,256,256]{2,1,0:T(8,128)(2,1)S(1)}, ...), branch_computations={%region_41.42_spmd, %region_42.43_spmd} | conditional | flops 269090816 | bytes 6029320
  (277 shorter events, 164.9 us)
Async XLA Ops:
  0.6 220.8 %copy-start = (f32[8]{0:T(128)S(1)}, f32[8]{0:T(128)}, u32[]{:S(2)}) copy-start(f32[8]{0:T(128)} %param.51) | copy-start | bytes 100
  1.7 36.6 %collective-permute-start.4 = (bf16[2,256,256]{2,1,0:T(8,128)(2,1)S(1)}, bf16[2,256,256]{2,1,0:T(8,128)(2,1)S(1)}, u32[]{:S(2)}, u32[]{:S(2)}) collective-permute-start(bf16[2,256,256]{2,1,0:T(8,128)(2,1)S(1)} %constant_dynamic-slice_fusion), channel_id=1, source_target_pairs={{0,2},{1,3},{2,0},{3,1},{4,6},{5,7},{6,4},{7,5},{8,10},{9,11},{10,... | collective-permute-start | bytes 786440 | tf_op jit(solution)/shard_map/ppermute | solution.py:11
  7.2 11.6 %collective-permute-start.1 = (bf16[2,256,256]{2,1,0:T(8,128)(2,1)S(1)}, bf16[2,256,256]{2,1,0:T(8,128)(2,1)S(1)}, u32[]{:S(2)}, u32[]{:S(2)}) collective-permute-start(bf16[2,256,256]{2,1,0:T(8,128)(2,1)S(1)} %constant_dynamic-slice_fusion), channel_id=1, source_target_pairs={{0,1},{1,0},{2,3},{3,2},{4,5},{5,4},{6,7},{7,6},{8,9},{9,8},{10,11... | collective-permute-start | bytes 786440 | tf_op jit(solution)/shard_map/ppermute | solution.py:11
  10.6 11.4 %collective-permute-start = (bf16[2,256,256]{2,1,0:T(8,128)(2,1)S(1)}, bf16[2,256,256]{2,1,0:T(8,128)(2,1)S(1)}, u32[]{:S(2)}, u32[]{:S(2)}) collective-permute-start(bf16[2,256,256]{2,1,0:T(8,128)(2,1)S(1)} %get-tuple-element.674), channel_id=1, source_target_pairs={{0,2},{1,3},{2,0},{3,1},{4,6},{5,7},{6,4},{7,5},{8,10},{9,11},{10,... | collective-permute-start | bytes 786440 | tf_op jit(solution)/shard_map/ppermute | solution.py:11
  15.6 19.2 %collective-permute-start.7 = (bf16[2,256,256]{2,1,0:T(8,128)(2,1)S(1)}, bf16[2,256,256]{2,1,0:T(8,128)(2,1)S(1)}, u32[]{:S(2)}, u32[]{:S(2)}) collective-permute-start(bf16[2,256,256]{2,1,0:T(8,128)(2,1)S(1)} %pad_maximum_fusion.41), channel_id=1, source_target_pairs={{0,1},{1,0},{2,3},{3,2},{4,5},{5,4},{6,7},{7,6},{8,9},{9,8},{10,11... | collective-permute-start | bytes 786440 | tf_op jit(solution)/shard_map/ppermute | solution.py:11
  23.6 14.7 %collective-permute-start.3 = (bf16[2,256,256]{2,1,0:T(8,128)(2,1)S(1)}, bf16[2,256,256]{2,1,0:T(8,128)(2,1)S(1)}, u32[]{:S(2)}, u32[]{:S(2)}) collective-permute-start(bf16[2,256,256]{2,1,0:T(8,128)(2,1)S(1)} %get-tuple-element.678), channel_id=1, source_target_pairs={{0,1},{1,0},{2,3},{3,2},{4,5},{5,4},{6,7},{7,6},{8,9},{9,8},{10,11... | collective-permute-start | bytes 786440 | tf_op jit(solution)/shard_map/ppermute | solution.py:11
  27.5 20.7 %collective-permute-start.2 = (bf16[2,256,256]{2,1,0:T(8,128)(2,1)S(1)}, bf16[2,256,256]{2,1,0:T(8,128)(2,1)}, u32[]{:S(2)}, u32[]{:S(2)}) collective-permute-start(bf16[2,256,256]{2,1,0:T(8,128)(2,1)S(1)} %pad_maximum_fusion.41), channel_id=1, source_target_pairs={{0,2},{1,3},{2,0},{3,1},{4,6},{5,7},{6,4},{7,5},{8,10},{9,11},{10,... | collective-permute-start | bytes 786440 | tf_op jit(solution)/shard_map/ppermute | solution.py:11
  32.8 25.8 %collective-permute-start.5 = (bf16[2,256,256]{2,1,0:T(8,128)(2,1)S(1)}, bf16[2,256,256]{2,1,0:T(8,128)(2,1)S(1)}, u32[]{:S(2)}, u32[]{:S(2)}) collective-permute-start(bf16[2,256,256]{2,1,0:T(8,128)(2,1)S(1)} %get-tuple-element.673), channel_id=1, source_target_pairs={{0,2},{1,3},{2,0},{3,1},{4,6},{5,7},{6,4},{7,5},{8,10},{9,11},{10,... | collective-permute-start | bytes 786440 | tf_op jit(solution)/shard_map/ppermute | solution.py:11
  36.4 12.9 %collective-permute-start.8 = (bf16[2,256,256]{2,1,0:T(8,128)(2,1)S(1)}, bf16[2,256,256]{2,1,0:T(8,128)(2,1)S(1)}, u32[]{:S(2)}, u32[]{:S(2)}) collective-permute-start(bf16[2,256,256]{2,1,0:T(8,128)(2,1)S(1)} %get-tuple-element.682), channel_id=1, source_target_pairs={{0,1},{1,0},{2,3},{3,2},{4,5},{5,4},{6,7},{7,6},{8,9},{9,8},{10,11... | collective-permute-start | bytes 786440 | tf_op jit(solution)/shard_map/ppermute | solution.py:11
  39.9 18.7 %collective-permute-start.6 = (bf16[2,256,256]{2,1,0:T(8,128)(2,1)S(1)}, bf16[2,256,256]{2,1,0:T(8,128)(2,1)S(1)}, u32[]{:S(2)}, u32[]{:S(2)}) collective-permute-start(bf16[2,256,256]{2,1,0:T(8,128)(2,1)S(1)} %get-tuple-element.680), channel_id=1, source_target_pairs={{0,1},{1,0},{2,3},{3,2},{4,5},{5,4},{6,7},{7,6},{8,9},{9,8},{10,11... | collective-permute-start | bytes 786440 | tf_op jit(solution)/shard_map/ppermute | solution.py:11
  43.3 30.6 %collective-permute-start.11 = (bf16[2,256,256]{2,1,0:T(8,128)(2,1)S(1)}, bf16[2,256,256]{2,1,0:T(8,128)(2,1)}, u32[]{:S(2)}, u32[]{:S(2)}) collective-permute-start(bf16[2,256,256]{2,1,0:T(8,128)(2,1)S(1)} %get-tuple-element.680), channel_id=1, source_target_pairs={{0,2},{1,3},{2,0},{3,1},{4,6},{5,7},{6,4},{7,5},{8,10},{9,11},{10,... | collective-permute-start | bytes 786440 | tf_op jit(solution)/shard_map/ppermute | solution.py:11
  54.5 14.5 %collective-permute-start.14 = (bf16[2,256,256]{2,1,0:T(8,128)(2,1)S(1)}, bf16[2,256,256]{2,1,0:T(8,128)(2,1)S(1)}, u32[]{:S(2)}, u32[]{:S(2)}) collective-permute-start(bf16[2,256,256]{2,1,0:T(8,128)(2,1)S(1)} %get-tuple-element.683), channel_id=1, source_target_pairs={{0,1},{1,0},{2,3},{3,2},{4,5},{5,4},{6,7},{7,6},{8,9},{9,8},{10,11... | collective-permute-start | bytes 786440 | tf_op jit(solution)/shard_map/ppermute | solution.py:11
  60.2 13.7 %collective-permute-start.10 = (bf16[2,256,256]{2,1,0:T(8,128)(2,1)S(1)}, bf16[2,256,256]{2,1,0:T(8,128)(2,1)S(1)}, u32[]{:S(2)}, u32[]{:S(2)}) collective-permute-start(bf16[2,256,256]{2,1,0:T(8,128)(2,1)S(1)} %get-tuple-element.681), channel_id=1, source_target_pairs={{0,1},{1,0},{2,3},{3,2},{4,5},{5,4},{6,7},{7,6},{8,9},{9,8},{10,11... | collective-permute-start | bytes 786440 | tf_op jit(solution)/shard_map/ppermute | solution.py:11
  62.1 35.9 %collective-permute-start.12 = (bf16[2,256,256]{2,1,0:T(8,128)(2,1)S(1)}, bf16[2,256,256]{2,1,0:T(8,128)(2,1)S(1)}, u32[]{:S(2)}, u32[]{:S(2)}) collective-permute-start(bf16[2,256,256]{2,1,0:T(8,128)(2,1)S(1)} %get-tuple-element.675), channel_id=1, source_target_pairs={{0,2},{1,3},{2,0},{3,1},{4,6},{5,7},{6,4},{7,5},{8,10},{9,11},{10,... | collective-permute-start | bytes 786440 | tf_op jit(solution)/shard_map/ppermute | solution.py:11
  64.4 19.7 %collective-permute-start.9 = (bf16[2,256,256]{2,1,0:T(8,128)(2,1)S(1)}, bf16[2,256,256]{2,1,0:T(8,128)(2,1)}, u32[]{:S(2)}, u32[]{:S(2)}) collective-permute-start(bf16[2,256,256]{2,1,0:T(8,128)(2,1)S(1)} %get-tuple-element.683), channel_id=1, source_target_pairs={{0,2},{1,3},{2,0},{3,1},{4,6},{5,7},{6,4},{7,5},{8,10},{9,11},{10,... | collective-permute-start | bytes 786440 | tf_op jit(solution)/shard_map/ppermute | solution.py:11
  70.6 18.0 %collective-permute-start.15 = (bf16[2,256,256]{2,1,0:T(8,128)(2,1)S(1)}, bf16[2,256,256]{2,1,0:T(8,128)(2,1)S(1)}, u32[]{:S(2)}, u32[]{:S(2)}) collective-permute-start(bf16[2,256,256]{2,1,0:T(8,128)(2,1)S(1)} %get-tuple-element.687), channel_id=1, source_target_pairs={{0,1},{1,0},{2,3},{3,2},{4,5},{5,4},{6,7},{7,6},{8,9},{9,8},{10,11... | collective-permute-start | bytes 786440 | tf_op jit(solution)/shard_map/ppermute | solution.py:11
  79.2 18.9 %collective-permute-start.13 = (bf16[2,256,256]{2,1,0:T(8,128)(2,1)S(1)}, bf16[2,256,256]{2,1,0:T(8,128)(2,1)}, u32[]{:S(2)}, u32[]{:S(2)}) collective-permute-start(bf16[2,256,256]{2,1,0:T(8,128)(2,1)S(1)} %get-tuple-element.685), channel_id=1, source_target_pairs={{0,1},{1,0},{2,3},{3,2},{4,5},{5,4},{6,7},{7,6},{8,9},{9,8},{10,11... | collective-permute-start | bytes 786440 | tf_op jit(solution)/shard_map/ppermute | solution.py:11
  81.1 40.3 %collective-permute-start.18 = (bf16[2,256,256]{2,1,0:T(8,128)(2,1)S(1)}, bf16[2,256,256]{2,1,0:T(8,128)(2,1)}, u32[]{:S(2)}, u32[]{:S(2)}) collective-permute-start(bf16[2,256,256]{2,1,0:T(8,128)(2,1)S(1)} %get-tuple-element.685), channel_id=1, source_target_pairs={{0,2},{1,3},{2,0},{3,1},{4,6},{5,7},{6,4},{7,5},{8,10},{9,11},{10,... | collective-permute-start | bytes 786440 | tf_op jit(solution)/shard_map/ppermute | solution.py:11
  93.8 18.4 %collective-permute-start.21 = (bf16[2,256,256]{2,1,0:T(8,128)(2,1)S(1)}, bf16[2,256,256]{2,1,0:T(8,128)(2,1)}, u32[]{:S(2)}, u32[]{:S(2)}) collective-permute-start(bf16[2,256,256]{2,1,0:T(8,128)(2,1)S(1)} %get-tuple-element.688), channel_id=1, source_target_pairs={{0,1},{1,0},{2,3},{3,2},{4,5},{5,4},{6,7},{7,6},{8,9},{9,8},{10,11... | collective-permute-start | bytes 786440 | tf_op jit(solution)/shard_map/ppermute | solution.py:11
  103.4 18.0 %collective-permute-start.17 = (bf16[2,256,256]{2,1,0:T(8,128)(2,1)S(1)}, bf16[2,256,256]{2,1,0:T(8,128)(2,1)}, u32[]{:S(2)}, u32[]{:S(2)}) collective-permute-start(bf16[2,256,256]{2,1,0:T(8,128)(2,1)S(1)} %get-tuple-element.686), channel_id=1, source_target_pairs={{0,1},{1,0},{2,3},{3,2},{4,5},{5,4},{6,7},{7,6},{8,9},{9,8},{10,11... | collective-permute-start | bytes 786440 | tf_op jit(solution)/shard_map/ppermute | solution.py:11
  105.4 41.1 %collective-permute-start.19 = (bf16[2,256,256]{2,1,0:T(8,128)(2,1)S(1)}, bf16[2,256,256]{2,1,0:T(8,128)(2,1)S(1)}, u32[]{:S(2)}, u32[]{:S(2)}) collective-permute-start(bf16[2,256,256]{2,1,0:T(8,128)(2,1)S(1)} %get-tuple-element.672), channel_id=1, source_target_pairs={{0,2},{1,3},{2,0},{3,1},{4,6},{5,7},{6,4},{7,5},{8,10},{9,11},{10,... | collective-permute-start | bytes 786440 | tf_op jit(solution)/shard_map/ppermute | solution.py:11
  107.7 28.0 %collective-permute-start.16 = (bf16[2,256,256]{2,1,0:T(8,128)(2,1)S(1)}, bf16[2,256,256]{2,1,0:T(8,128)(2,1)}, u32[]{:S(2)}, u32[]{:S(2)}) collective-permute-start(bf16[2,256,256]{2,1,0:T(8,128)(2,1)S(1)} %get-tuple-element.688), channel_id=1, source_target_pairs={{0,2},{1,3},{2,0},{3,1},{4,6},{5,7},{6,4},{7,5},{8,10},{9,11},{10,... | collective-permute-start | bytes 786440 | tf_op jit(solution)/shard_map/ppermute | solution.py:11
  118.1 17.6 %collective-permute-start.22 = (bf16[2,256,256]{2,1,0:T(8,128)(2,1)}, bf16[2,256,256]{2,1,0:T(8,128)(2,1)S(1)}, u32[]{:S(2)}, u32[]{:S(2)}) collective-permute-start(bf16[2,256,256]{2,1,0:T(8,128)(2,1)} %get-tuple-element.692), channel_id=1, source_target_pairs={{0,1},{1,0},{2,3},{3,2},{4,5},{5,4},{6,7},{7,6},{8,9},{9,8},{10,11... | collective-permute-start | bytes 786440 | tf_op jit(solution)/shard_map/ppermute | solution.py:11
  126.9 19.5 %collective-permute-start.20 = (bf16[2,256,256]{2,1,0:T(8,128)(2,1)S(1)}, bf16[2,256,256]{2,1,0:T(8,128)(2,1)}, u32[]{:S(2)}, u32[]{:S(2)}) collective-permute-start(bf16[2,256,256]{2,1,0:T(8,128)(2,1)S(1)} %get-tuple-element.690), channel_id=1, source_target_pairs={{0,1},{1,0},{2,3},{3,2},{4,5},{5,4},{6,7},{7,6},{8,9},{9,8},{10,11... | collective-permute-start | bytes 786440 | tf_op jit(solution)/shard_map/ppermute | solution.py:11
  144.5 35.5 %collective-permute-start.23 = (bf16[2,256,256]{2,1,0:T(8,128)(2,1)S(1)}, bf16[2,256,256]{2,1,0:T(8,128)(2,1)}, u32[]{:S(2)}, u32[]{:S(2)}) collective-permute-start(bf16[2,256,256]{2,1,0:T(8,128)(2,1)S(1)} %get-tuple-element.693), channel_id=1, source_target_pairs={{0,2},{1,3},{2,0},{3,1},{4,6},{5,7},{6,4},{7,5},{8,10},{9,11},{10,... | collective-permute-start | bytes 786440 | tf_op jit(solution)/shard_map/ppermute | solution.py:11
  151.7 28.3 %collective-permute-start.24 = (bf16[2,256,256]{2,1,0:T(8,128)(2,1)S(1)}, bf16[2,256,256]{2,1,0:T(8,128)(2,1)}, u32[]{:S(2)}, u32[]{:S(2)}) collective-permute-start(bf16[2,256,256]{2,1,0:T(8,128)(2,1)S(1)} %get-tuple-element.691), channel_id=1, source_target_pairs={{0,1},{1,0},{2,3},{3,2},{4,5},{5,4},{6,7},{7,6},{8,9},{9,8},{10,11... | collective-permute-start | bytes 786440 | tf_op jit(solution)/shard_map/ppermute | solution.py:11
  189.6 17.5 %copy-start.6 = (s32[8]{0:T(128)S(1)}, s32[8]{0:T(128)}, u32[]{:S(2)}) copy-start(s32[8]{0:T(128)} %param.49) | copy-start | bytes 100
  190.5 29.2 %all-to-all-start = ((bf16[32,1,2,16,256]{4,3,2,1,0:T(8,128)(2,1)}), bf16[32,1,2,16,256]{4,3,2,1,0:T(8,128)(2,1)S(1)}, u32[]{:S(2)}, u32[]{:S(2)}) async-start(bf16[32,1,2,16,256]{4,3,2,1,0:T(8,128)(2,1)} %copy.23), calls=%async_computation | async-start | bytes 1048576 | tf_op jit(solution)/shard_map/all_to_all | solution.py:117
  223.2 47.9 %all-to-all-start.1 = ((bf16[16,1,2,16,512]{4,3,2,1,0:T(8,128)(2,1)}), bf16[16,1,2,16,512]{4,3,2,1,0:T(8,128)(2,1)S(1)}, u32[]{:S(2)}, u32[]{:S(2)}) async-start(bf16[16,1,2,16,512]{4,3,2,1,0:T(8,128)(2,1)} %broadcast_in_dim.47), calls=%async_computation.1 | async-start | bytes 1048576 | tf_op jit(solution)/shard_map/all_to_all | solution.py:16
  242.5 9.6 %collective-permute-start.26 = (bf16[2,256,256]{2,1,0:T(8,128)(2,1)S(1)}, bf16[2,256,256]{2,1,0:T(8,128)(2,1)S(1)}, u32[]{:S(2)}, u32[]{:S(2)}) collective-permute-start(bf16[2,256,256]{2,1,0:T(8,128)(2,1)S(1)} %get-tuple-element.693), channel_id=1, source_target_pairs={{0,1},{1,0},{2,3},{3,2},{4,5},{5,4},{6,7},{7,6},{8,9},{9,8},{10,11... | collective-permute-start | bytes 786440 | tf_op jit(solution)/shard_map/ppermute | solution.py:11
  244.7 14.3 %collective-permute-start.25 = (bf16[2,256,256]{2,1,0:T(8,128)(2,1)S(1)}, bf16[2,256,256]{2,1,0:T(8,128)(2,1)S(1)}, u32[]{:S(2)}, u32[]{:S(2)}) collective-permute-start(bf16[2,256,256]{2,1,0:T(8,128)(2,1)S(1)} %get-tuple-element.690), channel_id=1, source_target_pairs={{0,2},{1,3},{2,0},{3,1},{4,6},{5,7},{6,4},{7,5},{8,10},{9,11},{10,... | collective-permute-start | bytes 786440 | tf_op jit(solution)/shard_map/ppermute | solution.py:11
  253.7 10.5 %collective-permute-start.27 = (bf16[2,256,256]{2,1,0:T(8,128)(2,1)S(1)}, bf16[2,256,256]{2,1,0:T(8,128)(2,1)S(1)}, u32[]{:S(2)}, u32[]{:S(2)}) collective-permute-start(bf16[2,256,256]{2,1,0:T(8,128)(2,1)S(1)} %get-tuple-element.696), channel_id=1, source_target_pairs={{0,1},{1,0},{2,3},{3,2},{4,5},{5,4},{6,7},{7,6},{8,9},{9,8},{10,11... | collective-permute-start | bytes 786440 | tf_op jit(solution)/shard_map/ppermute | solution.py:11
  (5 other events, 13.2 us)
where the time goes:
time: 274 us; the launch traced here: 272 us
  starting transfers between devices  127 us (46%)
  matrix products  89.5 us (33%)
  waiting for transfers between devices  29.3 us (11%)
  local copies, waits for them, and re-layouts  17.6 us (6%)
  other arithmetic  5.54 us (2%)
    ppermute x28, starting transfers between devices, partner(): lax.ppermute(shard, axis, [(i, i ^ 1 << stride) for i in range(lax.axis_s...  90.7 us
    dot_general x160, matrix products, single(): return jnp.dot(leading, trailing, preferred_element_type=jnp.float32)  84.7 us
    all_to_all x1, starting transfers between devices, from_everyone(): return lax.all_to_all(copies, axis, split_axis=0, concat_axis=0, tiled=True)  19.4 us
    ppermute x28, waiting for transfers between devices, partner(): lax.ppermute(shard, axis, [(i, i ^ 1 << stride) for i in range(lax.axis_s...  16.8 us
    all_to_all x1, starting transfers between devices, local(): lax.all_to_all(partial_terms[:, None].astype(jnp.bfloat16), 'rows', split...  16.5 us
    all_to_all x1, waiting for transfers between devices, local(): lax.all_to_all(partial_terms[:, None].astype(jnp.bfloat16), 'rows', split...  12.5 us
  transfers between devices with their start and end apart: 30, of which 8 were waited for; matrix products, arithmetic and copies ran while one was open for 35% of the time, Pallas kernels for 0%

commit v1 on v0

v1 whole, which is shorter than its diff:
```python
import jax
import jax.numpy as jnp
from jax import lax
from jax.experimental import pallas as pl
from jax.experimental.pallas import tpu as pltpu
from jax.sharding import PartitionSpec as P


ITERS = 4
CHUNK = 2
FLIPS = (1, 3, 2)
VMEM_WHOLE = pl.BlockSpec(memory_space=pltpu.VMEM)
SMEM_WHOLE = pl.BlockSpec(memory_space=pltpu.SMEM)
HBM_WHOLE = pl.BlockSpec(memory_space=pltpu.HBM)
MIB = 1 << 20


def dot(left, right):
    return jnp.dot(left, right, preferred_element_type=jnp.float32)


def row_bit():
    return lax.rem(lax.div(lax.axis_index("rows"), 2), 2)


def core_bit():
    return lax.rem(lax.axis_index("energy"), 2)


def embed(ref, rows, columns, real, imag):
    high = ref.shape[0] // 2
    wide = ref.shape[1] // 2
    (r0, r1), (c0, c1) = rows, columns
    ref[r0:r1, c0:c1] = real
    ref[high + r0 : high + r1, c0:c1] = imag
    ref[r0:r1, wide + c0 : wide + c1] = -imag
    ref[high + r0 : high + r1, wide + c0 : wide + c1] = real


def prepare(row_ref, coupling_ref, states_ref, forward_ref, backward_ref, drive_ref, sums):
    order = coupling_ref.shape[-1]
    whole = ((0, order), (0, order))
    real, imag = coupling_ref[0], coupling_ref[1]
    embed(forward_ref, *whole, real, imag)
    embed(backward_ref, *whole, real.T, -imag.T)
    sums[...] = jnp.zeros_like(sums)
    for contact in range(states_ref.shape[0]):
        row = row_ref[contact]
        sums[row] = sums[row] + states_ref[contact].astype(jnp.float32)
    drive = sums[...].astype(jnp.bfloat16)
    block_rows, _, count, _ = drive.shape
    count = block_rows * count
    embed(
        drive_ref,
        (0, count),
        (0, order),
        drive[:, 0].reshape(count, order),
        drive[:, 1].reshape(count, order),
    )


def assemble(step, fetched, green):
    row, column = row_bit(), core_bit()
    own_ref, side_ref, cross_ref, down_ref = fetched
    half = own_ref.shape[-1]
    for blocks, a, b in (
        (own_ref, row, column),
        (side_ref, row, 1 - column),
        (cross_ref, 1 - row, 1 - column),
        (down_ref, 1 - row, column),
    ):
        for part in range(2):
            start = pl.multiple_of(part * 2 * half + a * half, half)
            green[b, pl.ds(start, half), :] = blocks[step, part]


def own_rows(matrix, part):
    half = matrix.shape[0] // 4
    start = pl.multiple_of(part * 2 * half + row_bit() * half, half)
    return matrix[pl.ds(start, half), :]


def step_products(source, target, green, products, surface_from, surface):
    order = source[0].shape[0] // 2
    half = order // 2
    for coupling, product in zip(source, products):
        for b in range(2):
            value = dot(coupling[...], green[b]).astype(jnp.bfloat16)
            embed(product, (0, order), (b * half, (b + 1) * half), value[:order], value[order:])
    for part in range(2):
        term = dot(own_rows(products[0], part), source[1][:, :order])
        surface[part] = term if surface_from is None else surface_from[part] + term
    for product, coupling, following in zip(products, source, target):
        for b in range(2):
            columns = (b * half, (b + 1) * half)
            value = dot(product[...], coupling[:, columns[0] : columns[1]]).astype(jnp.bfloat16)
            embed(following, (0, order), columns, value[:order], value[order:])


def first_steps(
    forward_in, backward_in, own_ref, side_ref, cross_ref, down_ref,
    forward, backward, surface, green, forward_green, backward_green,
):
    source, target = (forward_in, backward_in), (forward, backward)
    surface_from = None
    for step in range(CHUNK):
        assemble(step, (own_ref, side_ref, cross_ref, down_ref), green)
        step_products(source, target, green, (forward_green, backward_green), surface_from, surface)
        source, surface_from = target, surface


def last_steps(
    forward_in, backward_in, surface_in, drive_ref, own_ref, side_ref, cross_ref, down_ref,
    forward_out, backward_out, green_out, forward_rows_out, injected,
    forward, backward, green, forward_rows, surface, forward_green, backward_green, copy_sems,
):
    fetched = (own_ref, side_ref, cross_ref, down_ref)
    leaving = (forward, backward, green, forward_rows)
    outs = (forward_out, backward_out, green_out, forward_rows_out)
    copies = [
        pltpu.make_async_copy(kept, out, copy_sems.at[i])
        for i, (kept, out) in enumerate(zip(leaving, outs))
    ]
    source, target = (forward_in, backward_in), (forward, backward)
    surface_from = surface_in
    for step in range(CHUNK - 1):
        assemble(step, fetched, green)
        step_products(source, target, green, (forward_green, backward_green), surface_from, surface)
        source, surface_from = target, surface
    copies[0].start()
    copies[1].start()
    assemble(CHUNK - 1, fetched, green)
    copies[2].start()
    order = forward.shape[0] // 2
    half = order // 2
    for b in range(2):
        columns = (b * half, (b + 1) * half)
        real = dot(own_rows(forward, 0), green[b]).astype(jnp.bfloat16)
        imag = dot(own_rows(forward, 1), green[b]).astype(jnp.bfloat16)
        embed(forward_rows, (0, half), columns, real, imag)
    copies[3].start()
    energy = []
    for part in range(2):
        rows = forward_rows[part * half : (part + 1) * half, :]
        energy.append((surface[part] + dot(rows, backward[:, :order])).astype(jnp.bfloat16))
    value = lax.dot_general(
        drive_ref[...],
        jnp.concatenate(energy, axis=1),
        (((1,), (1,)), ((), ())),
        preferred_element_type=jnp.float32,
    ).astype(jnp.bfloat16)
    block_rows, _, count, _ = injected.shape
    rows = block_rows * count
    for part in range(2):
        injected[:, part] = value[part * rows : (part + 1) * rows].reshape(block_rows, count, half)
    for copy in copies:
        copy.wait()


def far_blocks(forward, backward, green, forward_rows, kept_ref, given_ref, backward_rows):
    order = forward.shape[0] // 2
    half = order // 2
    core = core_bit()
    for b in range(2):
        columns = (b * half, (b + 1) * half)
        real = dot(own_rows(backward, 0), green[b]).astype(jnp.bfloat16)
        imag = dot(own_rows(backward, 1), green[b]).astype(jnp.bfloat16)
        embed(backward_rows, (0, half), columns, real, imag)
    for which, rows, coupling in ((0, forward_rows, forward), (1, backward_rows, backward)):
        for b in range(2):
            for part in range(2):
                value = dot(
                    rows[part * half : (part + 1) * half, :],
                    coupling[:, b * half : (b + 1) * half],
                ).astype(jnp.bfloat16)

                @pl.when(core == b)
                def _():
                    kept_ref[which, part] = value

                @pl.when(core != b)
                def _():
                    given_ref[which, part] = value


def spread(assignment_ref, weight_ref, received_ref, injection_ref, weighted_ref):
    groups = injection_ref.shape[0]
    half = received_ref.shape[-1]
    column = core_bit()
    for part in range(2):
        for a in range(2):
            total = jnp.zeros(injection_ref.shape[2:3] + (half,), jnp.float32)
            for slot in range(groups):
                e = lax.rem(assignment_ref[slot], groups)
                value = received_ref[slot, a, column, part].astype(jnp.float32)
                injection_ref[e, part, :, a * half : (a + 1) * half] = value
                total = total + weight_ref[e] * value
            total = total.astype(weighted_ref.dtype)
            for copy in range(weighted_ref.shape[0]):
                weighted_ref[copy, part, :, a * half : (a + 1) * half] = total


def call(body, outs, scratch, scalars=0, vmem=32, far_outs=0):
    def run(*operands):
        specs = [SMEM_WHOLE] * scalars + [VMEM_WHOLE] * (len(operands) - scalars)
        return pl.pallas_call(
            body,
            out_shape=outs,
            in_specs=specs,
            out_specs=tuple(HBM_WHOLE if i < far_outs else VMEM_WHOLE for i in range(len(outs))),
            scratch_shapes=scratch,
            compiler_params=pltpu.CompilerParams(vmem_limit_bytes=vmem * MIB),
        )(*operands)

    return run


def local(energies_axis, rows_axis, coupling, inverses, contact_row, assignment, states, weights):
    half = inverses.shape[-1]
    order = 2 * half
    slots = rows_axis // 4
    bf16, f32 = jnp.bfloat16, jnp.float32
    both = ("energy", "rows")

    def routes(flip, to_worker):
        pairs = []
        for energy in range(energies_axis):
            for slot in range(slots):
                for x in range(4):
                    if (x % 2 == energy % 2) == to_worker:
                        base = energy * rows_axis + slot * 4
                        pairs.append((base + (x ^ flip), base + x))
        return pairs

    chunks = [inverses[0, CHUNK * c : CHUNK * (c + 1)] for c in range(ITERS // CHUNK)]
    fetched = []
    for c, chunk in enumerate(chunks):
        fetched.append([])
        for flip in FLIPS:
            fetched[c].append(lax.ppermute(chunk, both, routes(flip, True)))

    square = jax.ShapeDtypeStruct((2 * order, 2 * order), bf16)
    count = states.shape[2]
    block_rows = rows_axis
    forward, backward, drive = call(
        prepare,
        (square, square, jax.ShapeDtypeStruct((2 * block_rows * count, 2 * order), bf16)),
        [pltpu.VMEM((block_rows, 2, count, order), f32)],
        scalars=1,
    )(contact_row, coupling, states)

    square_scratch = pltpu.VMEM((2 * order, 2 * order), bf16)
    green_shape = (2, 2 * order, half)
    surface_shape = (2, half, order)
    forward, backward, surface = call(
        first_steps,
        (square, square, jax.ShapeDtypeStruct(surface_shape, f32)),
        [pltpu.VMEM(green_shape, bf16), square_scratch, square_scratch],
    )(forward, backward, chunks[0], *fetched[0])
    forward, backward, green, forward_rows, injected = call(
        last_steps,
        (
            pltpu.HBM((2 * order, 2 * order), bf16),
            pltpu.HBM((2 * order, 2 * order), bf16),
            pltpu.HBM(green_shape, bf16),
            pltpu.HBM((order, 2 * order), bf16),
            jax.ShapeDtypeStruct((block_rows, 2, count, half), bf16),
        ),
        [
            square_scratch,
            square_scratch,
            pltpu.VMEM(green_shape, bf16),
            pltpu.VMEM((order, 2 * order), bf16),
            pltpu.VMEM(surface_shape, f32),
            square_scratch,
            square_scratch,
            pltpu.SemaphoreType.DMA((4,)),
        ],
        far_outs=4,
    )(forward, backward, surface, drive, chunks[1], *fetched[1])

    received = lax.all_to_all(injected, "rows", split_axis=0, concat_axis=0, tiled=True)

    far_shape = jax.ShapeDtypeStruct((2, 2, half, half), bf16)
    kept, given = call(
        far_blocks, (far_shape, far_shape), [pltpu.VMEM((order, 2 * order), bf16)]
    )(forward, backward, green, forward_rows)
    given = lax.ppermute(given, both, routes(1, False))
    worker = lax.axis_index("rows") % 2 == core_bit()
    far_out = jnp.where(worker, kept, given)

    groups = assignment.shape[0]
    chips = energies_axis // 2
    injection, weighted = call(
        spread,
        (
            jax.ShapeDtypeStruct((groups, 2, count, order), f32),
            jax.ShapeDtypeStruct((chips, 2, count, order), bf16),
        ),
        [],
        scalars=2,
    )(assignment, weights, received.reshape(slots, 2, 2, 2, count, half))
    alike = [[2 * chip + core for chip in range(chips)] for core in range(2)]
    gathered = lax.all_to_all(
        weighted, "energy", split_axis=0, concat_axis=0, axis_index_groups=alike, tiled=True
    )
    part_sum = jnp.sum(gathered.astype(f32), axis=0)
    other_sum = lax.ppermute(
        part_sum.astype(bf16), "energy", [(i, i ^ 1) for i in range(energies_axis)]
    )
    integrated = part_sum + other_sum.astype(f32)
    return injection[:, None], integrated[None], far_out[0][None], far_out[1][None]


def solution(mesh):
    def whole(*operands):
        return local(mesh.shape["energy"], mesh.shape["rows"], *operands)

    placed = (
        P(),
        P(("energy", "rows"), None, None, None, None),
        P(),
        P("energy"),
        P(),
        P("energy"),
    )
    return jax.shard_map(
        whole,
        mesh=mesh,
        in_specs=placed,
        out_specs=(
            P("energy", "rows", None, None, None),
            P("rows", None, None, None),
            P(("energy", "rows"), None, None, None),
            P(("energy", "rows"), None, None, None),
        ),
        check_vma=False,
    )
```

time: 274 us -> 98.7 us (0.36)
  matrix products: 89.5 us -> 0 us
  starting transfers between devices: 127 us -> 43.5 us
  Pallas kernels: 0 us -> 28.6 us
  waiting for transfers between devices: 29.3 us -> 15.3 us
  local copies, waits for them, and re-layouts: 17.6 us -> 9.07 us
  other arithmetic: 5.54 us -> 0.75 us
    dot_general x166 -> x0, matrix products: 89.5 us -> none  [the longest x160 84.7 us: single(): return jnp.dot(leading, trailing, preferred_element_type=jnp.float32)]
    ppermute x28 -> x8, starting transfers between devices: 90.7 us -> 21.2 us  [the longest x6 12.8 us: local(): fetched[c].append(lax.ppermute(chunk, both, routes(flip, True)))]
    pallas_call x0 -> x5, Pallas kernels: none -> 28.6 us  [run(): pl.pallas_call(body, out_shape=outs, in_specs=specs, out_specs=tuple((HBM...]
    all_to_all x2, starting transfers between devices: 35.9 us -> 22.3 us  [the longest x1 11.8 us: local(): lax.all_to_all(weighted, 'energy', split_axis=0, concat_axis=0, axis_inde...]
    ppermute x28 -> x8, waiting for transfers between devices: 16.8 us -> 3.73 us  [the longest x6 3.71 us: local(): fetched[c].append(lax.ppermute(chunk, both, routes(flip, True)))]
    dynamic_slice x3 -> x0, local copies, waits for them, and re-layouts: 4.36 us -> none  [the longest x2 3.37 us: local(): lax.dynamic_index_in_dim(drive, column_bit, axis=3, keepdims=False)]
    reshape x2 -> x0, local copies, waits for them, and re-layouts: 3.03 us -> none  [the longest x1 2.61 us: local(): drive = drive.reshape(block_rows, 2, states_count, 2, half_order)]
  transfers between devices with their start and end apart: 30 -> 10, of which waited for: 8 -> 4; matrix products, arithmetic and copies ran while one was open for 35% -> 1% of each run, Pallas kernels for 0% -> 17%
where the time goes in v1:
time: 98.7 us; the launch traced here: 98 us
  starting transfers between devices  43.5 us (44%)
  Pallas kernels  28.6 us (29%)
  waiting for transfers between devices  15.3 us (16%)
  local copies, waits for them, and re-layouts  9.07 us (9%)
    pallas_call x5, Pallas kernels, run(): pl.pallas_call(body, out_shape=outs, in_specs=specs, out_specs=tuple((HBM...  28.6 us
    ppermute x6, starting transfers between devices, local(): fetched[c].append(lax.ppermute(chunk, both, routes(flip, True)))  12.8 us
    all_to_all x1, starting transfers between devices, local(): lax.all_to_all(weighted, 'energy', split_axis=0, concat_axis=0, axis_inde...  11.8 us
    all_to_all x1, starting transfers between devices, local(): lax.all_to_all(injected, 'rows', split_axis=0, concat_axis=0, tiled=True)  10.5 us
    all_to_all x1, waiting for transfers between devices, local(): lax.all_to_all(weighted, 'energy', split_axis=0, concat_axis=0, axis_inde...  9.27 us
    ppermute x1, starting transfers between devices, local(): lax.ppermute(part_sum.astype(bf16), 'energy', [(i, i ^ 1) for i in range(...  7.05 us
    unnamed x18, local copies, waits for them, and re-layouts  6.86 us
    ppermute x6, waiting for transfers between devices, local(): fetched[c].append(lax.ppermute(chunk, both, routes(flip, True)))  3.71 us
  transfers between devices with their start and end apart: 10, of which 4 were waited for; matrix products, arithmetic and copies ran while one was open for 1% of the time, Pallas kernels for 17%

profile of v1, /device:TPU:1, one launch (start us, length us, event | category | flops | bytes accessed | tf_op | source)
XLA Modules:
  0.0 98.0 jit_solution(12911590191322119315)
XLA Ops:
  0.7 1.4 %slice_bitcast_fusion = (bf16[2,2,256,256]{3,2,1,0:T(8,128)(2,1)S(1)}, bf16[2,2,256,256]{3,2,1,0:T(8,128)(2,1)S(1)}) fusion(bf16[1,4,2,256,256]{4,3,2,1,0:T(8,128)(2,1)} %param.7), kind=kLoop, calls=%fused_computation.1 | loop fusion | bytes 2097152 | tf_op jit(solution)/shard_map/squeeze | solution.py:235
  2.0 4.0 %collective-permute-start = (bf16[2,2,256,256]{3,2,1,0:T(8,128)(2,1)S(1)}, bf16[2,2,256,256]{3,2,1,0:T(8,128)(2,1)S(1)}, u32[]{:S(2)}, u32[]{:S(2)}) collective-permute-start(bf16[2,2,256,256]{3,2,1,0:T(8,128)(2,1)S(1)} %get-tuple-element.39.own_ref), channel_id=1, source_target_pairs={{1,0},{3,2},{5,4},{7,6},{9,8},{11,10},{13,12},{15,14},{17,16},{19,... | collective-permute-start | bytes 1572872 | tf_op jit(solution)/shard_map/ppermute | solution.py:240
  6.0 2.6 %collective-permute-start.1 = (bf16[2,2,256,256]{3,2,1,0:T(8,128)(2,1)S(1)}, bf16[2,2,256,256]{3,2,1,0:T(8,128)(2,1)S(1)}, u32[]{:S(2)}, u32[]{:S(2)}) collective-permute-start(bf16[2,2,256,256]{3,2,1,0:T(8,128)(2,1)S(1)} %get-tuple-element.39.own_ref), channel_id=1, source_target_pairs={{3,0},{1,2},{7,4},{5,6},{11,8},{9,10},{15,12},{13,14},{19,16},{17,... | collective-permute-start | bytes 1572872 | tf_op jit(solution)/shard_map/ppermute | solution.py:240
  8.6 0.7 collective-permute-start.2
  9.3 3.1 %collective-permute-start.3 = (bf16[2,2,256,256]{3,2,1,0:T(8,128)(2,1)S(1)}, bf16[2,2,256,256]{3,2,1,0:T(8,128)(2,1)S(1)}, u32[]{:S(2)}, u32[]{:S(2)}) collective-permute-start(bf16[2,2,256,256]{3,2,1,0:T(8,128)(2,1)S(1)} %get-tuple-element.38.own_ref), channel_id=1, source_target_pairs={{1,0},{3,2},{5,4},{7,6},{9,8},{11,10},{13,12},{15,14},{17,16},{19,... | collective-permute-start | bytes 1572872 | tf_op jit(solution)/shard_map/ppermute | solution.py:240
  12.4 1.8 %collective-permute-start.4 = (bf16[2,2,256,256]{3,2,1,0:T(8,128)(2,1)S(1)}, bf16[2,2,256,256]{3,2,1,0:T(8,128)(2,1)S(1)}, u32[]{:S(2)}, u32[]{:S(2)}) collective-permute-start(bf16[2,2,256,256]{3,2,1,0:T(8,128)(2,1)S(1)} %get-tuple-element.38.own_ref), channel_id=1, source_target_pairs={{3,0},{1,2},{7,4},{5,6},{11,8},{9,10},{15,12},{13,14},{19,16},{17,... | collective-permute-start | bytes 1572872 | tf_op jit(solution)/shard_map/ppermute | solution.py:240
  14.2 0.0 collective-permute-done.side_ref
  14.2 0.7 collective-permute-start.5
  15.0 0.0 copy-start.3
  15.0 1.2 %copy-done.3 = bf16[2,512,512]{2,1,0:T(8,128)(2,1)S(1)} copy-done((bf16[2,512,512]{2,1,0:T(8,128)(2,1)S(1)}, bf16[2,512,512]{2,1,0:T(8,128)(2,1)}, u32[]{:S(2)}) %copy-start.3) | copy-done | bytes 1048600
  16.2 1.6 %shard_map.93 = (bf16[1024,1024]{1,0:T(8,128)(2,1)S(1)}, bf16[1024,1024]{1,0:T(8,128)(2,1)S(1)}, bf16[1024,1024]{1,0:T(8,128)(2,1)S(1)}) custom-call(s32[48]{0:T(128)S(1)} %copy-done.8, bf16[2,512,512]{2,1,0:T(8,128)(2,1)S(1)} %copy-done.3, bf16[48,2,16,512]{3,2,1,0:T(8,128)(2,1)S(1)} %copy-done.2), custom_call_target="tpu_custom_call" | custom-call | tf_op jit(solution)/shard_map/pallas_call | solution.py:206
  17.8 3.0 %collective-permute-done.1.cross_ref = bf16[2,2,256,256]{3,2,1,0:T(8,128)(2,1)S(1)} collective-permute-done((bf16[2,2,256,256]{3,2,1,0:T(8,128)(2,1)S(1)}, bf16[2,2,256,256]{3,2,1,0:T(8,128)(2,1)S(1)}, u32[]{:S(2)}, u32[]{:S(2)}) %collective-permute-start.1) | collective-permute-done | bytes 524320 | tf_op jit(solution)/shard_map/ppermute | solution.py:240
  20.7 10.0 %shard_map.94 = (bf16[1024,1024]{1,0:T(8,128)(2,1)S(1)}, bf16[1024,1024]{1,0:T(8,128)(2,1)S(1)}, f32[2,256,512]{2,1,0:T(8,128)S(1)}) custom-call(bf16[1024,1024]{1,0:T(8,128)(2,1)S(1)} %get-tuple-element.19.forward_in, bf16[1024,1024]{1,0:T(8,128)(2,1)S(1)} %get-tuple-element.20.backward_in, bf16[2,2,256,256]{3,2,1,0:T(8,128)(2,1)S(1)} %get-tuple-element.39.own_ref, ...), custom_call_target="tpu_custom_call" | custom-call | tf_op jit(solution)/shard_map/pallas_call | solution.py:206
  30.8 0.0 collective-permute-done.3.side_ref
  30.8 0.7 collective-permute-done.4.cross_ref
  31.5 11.5 %shard_map.95 = (bf16[1024,1024]{1,0:T(8,128)(2,1)}, bf16[1024,1024]{1,0:T(8,128)(2,1)}, bf16[2,1024,256]{2,1,0:T(8,128)(2,1)}, bf16[512,1024]{1,0:T(8,128)(2,1)}, bf16[32,2,16,256]{3,2,1,0:T(8,128)(2,1)}) custom-call(bf16[1024,1024]{1,0:T(8,128)(2,1)S(1)} %get-tuple-element.21.forward_in, bf16[1024,1024]{1,0:T(8,128)(2,1)S(1)} %get-tuple-element.22.backward_in, ...), custom_call_target="tpu_custom_call" | custom-call | tf_op jit(solution)/shard_map/pallas_call | solution.py:206
  43.0 10.5 %all-to-all-start = ((bf16[32,2,16,256]{3,2,1,0:T(8,128)(2,1)}), bf16[32,2,16,256]{3,2,1,0:T(8,128)(2,1)S(1)}, u32[]{:S(2)}, u32[]{:S(2)}) async-start(bf16[32,2,16,256]{3,2,1,0:T(8,128)(2,1)} %get-tuple-element.25), calls=%async_computation | async-start | bytes 1048576 | tf_op jit(solution)/shard_map/all_to_all | solution.py:282
  53.5 1.6 %copy-done = bf16[1024,1024]{1,0:T(8,128)(2,1)S(1)} copy-done((bf16[1024,1024]{1,0:T(8,128)(2,1)S(1)}, bf16[1024,1024]{1,0:T(8,128)(2,1)}, u32[]{:S(2)}) %copy-start) | copy-done | bytes 2097176
  55.1 1.6 %copy-done.1 = bf16[1024,1024]{1,0:T(8,128)(2,1)S(1)} copy-done((bf16[1024,1024]{1,0:T(8,128)(2,1)S(1)}, bf16[1024,1024]{1,0:T(8,128)(2,1)}, u32[]{:S(2)}) %copy-start.1) | copy-done | bytes 2097176
  56.7 1.2 %copy-done.4 = bf16[2,1024,256]{2,1,0:T(8,128)(2,1)S(1)} copy-done((bf16[2,1024,256]{2,1,0:T(8,128)(2,1)S(1)}, bf16[2,1024,256]{2,1,0:T(8,128)(2,1)}, u32[]{:S(2)}) %copy-start.4) | copy-done | bytes 1048600
  57.9 1.2 %copy-done.5 = bf16[512,1024]{1,0:T(8,128)(2,1)S(1)} copy-done((bf16[512,1024]{1,0:T(8,128)(2,1)S(1)}, bf16[512,1024]{1,0:T(8,128)(2,1)}, u32[]{:S(2)}) %copy-start.5) | copy-done | bytes 1048600
  59.1 4.0 %shard_map.97 = (bf16[2,2,256,256]{3,2,1,0:T(8,128)(2,1)S(1)}, bf16[2,2,256,256]{3,2,1,0:T(8,128)(2,1)S(1)}) custom-call(bf16[1024,1024]{1,0:T(8,128)(2,1)S(1)} %copy-done, bf16[1024,1024]{1,0:T(8,128)(2,1)S(1)} %copy-done.1, bf16[2,1024,256]{2,1,0:T(8,128)(2,1)S(1)} %copy-done.4, bf16[512,1024]{1,0:T(8,128)(2,1)S(1)} %copy-done.5), custom_call_target="tpu_custom_call" | custom-call | tf_op jit(solution)/shard_map/pallas_call | solution.py:206
  63.1 1.3 %collective-permute-start.7 = (bf16[2,2,256,256]{3,2,1,0:T(8,128)(2,1)S(1)}, bf16[2,2,256,256]{3,2,1,0:T(8,128)(2,1)S(1)}, u32[]{:S(2)}, u32[]{:S(2)}) collective-permute-start(bf16[2,2,256,256]{3,2,1,0:T(8,128)(2,1)S(1)} %get-tuple-element.33), channel_id=1, source_target_pairs={{0,1},{2,3},{4,5},{6,7},{8,9},{10,11},{12,13},{14,15},{16,17},{18,... | collective-permute-start | bytes 1572872 | tf_op jit(solution)/shard_map/ppermute | solution.py:288
  64.4 2.3 %all-to-all-done = bf16[32,2,16,256]{3,2,1,0:T(8,128)(2,1)S(1)} async-done(((bf16[32,2,16,256]{3,2,1,0:T(8,128)(2,1)}), bf16[32,2,16,256]{3,2,1,0:T(8,128)(2,1)S(1)}, u32[]{:S(2)}, u32[]{:S(2)}) %all-to-all-start) | async-done | bytes 524320 | tf_op jit(solution)/shard_map/all_to_all | solution.py:282
  66.8 1.5 %shard_map.96 = (f32[8,2,16,512]{3,2,1,0:T(8,128)}, bf16[8,2,16,512]{3,2,1,0:T(8,128)(2,1)}) custom-call(s32[8]{0:T(128)S(1)} %copy-done.6, f32[8]{0:T(128)S(1)} %copy-done.7, bf16[8,2,2,2,16,256]{5,4,3,2,1,0:T(8,128)(2,1)S(1)} %bitcast.10), custom_call_target="tpu_custom_call" | custom-call | tf_op jit(solution)/shard_map/pallas_call | solution.py:206
  68.3 11.8 %all-to-all-start.1 = ((bf16[8,2,16,512]{3,2,1,0:T(8,128)(2,1)}), bf16[8,2,16,512]{3,2,1,0:T(8,128)(2,1)S(1)}, u32[]{:S(2)}, u32[]{:S(2)}) async-start(bf16[8,2,16,512]{3,2,1,0:T(8,128)(2,1)} %get-tuple-element.27), calls=%async_computation.1 | async-start | bytes 524288 | tf_op jit(solution)/shard_map/all_to_all | solution.py:304
  80.1 0.1 broadcast_select_fusion
  80.2 9.3 %all-to-all-done.1 = bf16[8,2,16,512]{3,2,1,0:T(8,128)(2,1)S(1)} async-done(((bf16[8,2,16,512]{3,2,1,0:T(8,128)(2,1)}), bf16[8,2,16,512]{3,2,1,0:T(8,128)(2,1)S(1)}, u32[]{:S(2)}, u32[]{:S(2)}) %all-to-all-start.1) | async-done | bytes 262176 | tf_op jit(solution)/shard_map/all_to_all | solution.py:304
  89.5 7.1 %collective-permute-start.6 = (bf16[2,16,512]{2,1,0:T(8,128)(2,1)S(1)}, bf16[2,16,512]{2,1,0:T(8,128)(2,1)S(1)}, u32[]{:S(2)}, u32[]{:S(2)}) collective-permute-start(bf16[2,16,512]{2,1,0:T(8,128)(2,1)S(1)} %convert_element_type.10), channel_id=1, source_target_pairs={{0,32},{32,0},{64,96},{96,64},{128,160},{160,128},{192,224},{224,1... | collective-permute-start | bytes 98312 | tf_op jit(solution)/shard_map/ppermute | solution.py:308
  96.6 0.8 fusion
  97.4 0.0 collective-permute-done.6
  97.4 0.6 add_bitcast_fusion
  (17 shorter events, 0.1 us)
Async XLA Ops:
  0.6 14.3 %copy-start.2 = (bf16[48,2,16,512]{3,2,1,0:T(8,128)(2,1)S(1)}, bf16[48,2,16,512]{3,2,1,0:T(8,128)(2,1)}, u32[]{:S(2)}) copy-start(bf16[48,2,16,512]{3,2,1,0:T(8,128)(2,1)} %states_ref.1) | copy-start | bytes 4718596
  0.6 14.3 %copy-start.8 = (s32[48]{0:T(128)S(1)}, s32[48]{0:T(128)}, u32[]{:S(2)}) copy-start(s32[48]{0:T(128)} %row_ref.1) | copy-start | bytes 580
  2.0 12.2 %collective-permute-start = (bf16[2,2,256,256]{3,2,1,0:T(8,128)(2,1)S(1)}, bf16[2,2,256,256]{3,2,1,0:T(8,128)(2,1)S(1)}, u32[]{:S(2)}, u32[]{:S(2)}) collective-permute-start(bf16[2,2,256,256]{3,2,1,0:T(8,128)(2,1)S(1)} %get-tuple-element.39.own_ref), channel_id=1, source_target_pairs={{1,0},{3,2},{5,4},{7,6},{9,8},{11,10},{13,12},{15,14},{17,16},{19,... | collective-permute-start | bytes 1572872 | tf_op jit(solution)/shard_map/ppermute | solution.py:240
  6.0 14.7 %collective-permute-start.1 = (bf16[2,2,256,256]{3,2,1,0:T(8,128)(2,1)S(1)}, bf16[2,2,256,256]{3,2,1,0:T(8,128)(2,1)S(1)}, u32[]{:S(2)}, u32[]{:S(2)}) collective-permute-start(bf16[2,2,256,256]{3,2,1,0:T(8,128)(2,1)S(1)} %get-tuple-element.39.own_ref), channel_id=1, source_target_pairs={{3,0},{1,2},{7,4},{5,6},{11,8},{9,10},{15,12},{13,14},{19,16},{17,... | collective-permute-start | bytes 1572872 | tf_op jit(solution)/shard_map/ppermute | solution.py:240
  8.6 12.2 %collective-permute-start.2 = (bf16[2,2,256,256]{3,2,1,0:T(8,128)(2,1)S(1)}, bf16[2,2,256,256]{3,2,1,0:T(8,128)(2,1)S(1)}, u32[]{:S(2)}, u32[]{:S(2)}) collective-permute-start(bf16[2,2,256,256]{3,2,1,0:T(8,128)(2,1)S(1)} %get-tuple-element.39.own_ref), channel_id=1, source_target_pairs={{2,0},{0,2},{6,4},{4,6},{10,8},{8,10},{14,12},{12,14},{18,16},{16,... | collective-permute-start | bytes 1572872 | tf_op jit(solution)/shard_map/ppermute | solution.py:240
  9.3 21.5 %collective-permute-start.3 = (bf16[2,2,256,256]{3,2,1,0:T(8,128)(2,1)S(1)}, bf16[2,2,256,256]{3,2,1,0:T(8,128)(2,1)S(1)}, u32[]{:S(2)}, u32[]{:S(2)}) collective-permute-start(bf16[2,2,256,256]{3,2,1,0:T(8,128)(2,1)S(1)} %get-tuple-element.38.own_ref), channel_id=1, source_target_pairs={{1,0},{3,2},{5,4},{7,6},{9,8},{11,10},{13,12},{15,14},{17,16},{19,... | collective-permute-start | bytes 1572872 | tf_op jit(solution)/shard_map/ppermute | solution.py:240
  12.4 19.1 %collective-permute-start.4 = (bf16[2,2,256,256]{3,2,1,0:T(8,128)(2,1)S(1)}, bf16[2,2,256,256]{3,2,1,0:T(8,128)(2,1)S(1)}, u32[]{:S(2)}, u32[]{:S(2)}) collective-permute-start(bf16[2,2,256,256]{3,2,1,0:T(8,128)(2,1)S(1)} %get-tuple-element.38.own_ref), channel_id=1, source_target_pairs={{3,0},{1,2},{7,4},{5,6},{11,8},{9,10},{15,12},{13,14},{19,16},{17,... | collective-permute-start | bytes 1572872 | tf_op jit(solution)/shard_map/ppermute | solution.py:240
  14.2 17.3 %collective-permute-start.5 = (bf16[2,2,256,256]{3,2,1,0:T(8,128)(2,1)S(1)}, bf16[2,2,256,256]{3,2,1,0:T(8,128)(2,1)S(1)}, u32[]{:S(2)}, u32[]{:S(2)}) collective-permute-start(bf16[2,2,256,256]{3,2,1,0:T(8,128)(2,1)S(1)} %get-tuple-element.38.own_ref), channel_id=1, source_target_pairs={{2,0},{0,2},{6,4},{4,6},{10,8},{8,10},{14,12},{12,14},{18,16},{16,... | collective-permute-start | bytes 1572872 | tf_op jit(solution)/shard_map/ppermute | solution.py:240
  15.0 1.2 %copy-start.3 = (bf16[2,512,512]{2,1,0:T(8,128)(2,1)S(1)}, bf16[2,512,512]{2,1,0:T(8,128)(2,1)}, u32[]{:S(2)}) copy-start(bf16[2,512,512]{2,1,0:T(8,128)(2,1)} %coupling_ref.1) | copy-start | bytes 3145732
  43.0 23.8 %all-to-all-start = ((bf16[32,2,16,256]{3,2,1,0:T(8,128)(2,1)}), bf16[32,2,16,256]{3,2,1,0:T(8,128)(2,1)S(1)}, u32[]{:S(2)}, u32[]{:S(2)}) async-start(bf16[32,2,16,256]{3,2,1,0:T(8,128)(2,1)} %get-tuple-element.25), calls=%async_computation | async-start | bytes 1048576 | tf_op jit(solution)/shard_map/all_to_all | solution.py:282
  53.5 1.6 %copy-start = (bf16[1024,1024]{1,0:T(8,128)(2,1)S(1)}, bf16[1024,1024]{1,0:T(8,128)(2,1)}, u32[]{:S(2)}) copy-start(bf16[1024,1024]{1,0:T(8,128)(2,1)} %get-tuple-element.28.forward) | copy-start | bytes 6291460
  55.1 1.6 %copy-start.1 = (bf16[1024,1024]{1,0:T(8,128)(2,1)S(1)}, bf16[1024,1024]{1,0:T(8,128)(2,1)}, u32[]{:S(2)}) copy-start(bf16[1024,1024]{1,0:T(8,128)(2,1)} %get-tuple-element.29.backward) | copy-start | bytes 6291460
  56.7 1.2 %copy-start.4 = (bf16[2,1024,256]{2,1,0:T(8,128)(2,1)S(1)}, bf16[2,1024,256]{2,1,0:T(8,128)(2,1)}, u32[]{:S(2)}) copy-start(bf16[2,1024,256]{2,1,0:T(8,128)(2,1)} %get-tuple-element.30.green) | copy-start | bytes 3145732
  57.9 1.2 %copy-start.5 = (bf16[512,1024]{1,0:T(8,128)(2,1)S(1)}, bf16[512,1024]{1,0:T(8,128)(2,1)}, u32[]{:S(2)}) copy-start(bf16[512,1024]{1,0:T(8,128)(2,1)} %get-tuple-element.31.forward_rows) | copy-start | bytes 3145732
  59.1 7.6 %copy-start.6 = (s32[8]{0:T(128)S(1)}, s32[8]{0:T(128)}, u32[]{:S(2)}) copy-start(s32[8]{0:T(128)} %assignment_ref.1) | copy-start | bytes 100
  59.1 7.7 %copy-start.7 = (f32[8]{0:T(128)S(1)}, f32[8]{0:T(128)}, u32[]{:S(2)}) copy-start(f32[8]{0:T(128)} %weight_ref.1) | copy-start | bytes 100
  63.1 17.0 %collective-permute-start.7 = (bf16[2,2,256,256]{3,2,1,0:T(8,128)(2,1)S(1)}, bf16[2,2,256,256]{3,2,1,0:T(8,128)(2,1)S(1)}, u32[]{:S(2)}, u32[]{:S(2)}) collective-permute-start(bf16[2,2,256,256]{3,2,1,0:T(8,128)(2,1)S(1)} %get-tuple-element.33), channel_id=1, source_target_pairs={{0,1},{2,3},{4,5},{6,7},{8,9},{10,11},{12,13},{14,15},{16,17},{18,... | collective-permute-start | bytes 1572872 | tf_op jit(solution)/shard_map/ppermute | solution.py:288
  68.3 21.2 %all-to-all-start.1 = ((bf16[8,2,16,512]{3,2,1,0:T(8,128)(2,1)}), bf16[8,2,16,512]{3,2,1,0:T(8,128)(2,1)S(1)}, u32[]{:S(2)}, u32[]{:S(2)}) async-start(bf16[8,2,16,512]{3,2,1,0:T(8,128)(2,1)} %get-tuple-element.27), calls=%async_computation.1 | async-start | bytes 524288 | tf_op jit(solution)/shard_map/all_to_all | solution.py:304
  89.5 7.9 %collective-permute-start.6 = (bf16[2,16,512]{2,1,0:T(8,128)(2,1)S(1)}, bf16[2,16,512]{2,1,0:T(8,128)(2,1)S(1)}, u32[]{:S(2)}, u32[]{:S(2)}) collective-permute-start(bf16[2,16,512]{2,1,0:T(8,128)(2,1)S(1)} %convert_element_type.10), channel_id=1, source_target_pairs={{0,32},{32,0},{64,96},{96,64},{128,160},{160,128},{192,224},{224,1... | collective-permute-start | bytes 98312 | tf_op jit(solution)/shard_map/ppermute | solution.py:308

commit v2 on v1

--- a/solution.py
+++ b/solution.py
@@ -1,3 +1,5 @@
+import functools
+
 import jax
 import jax.numpy as jnp
 from jax import lax
@@ -27,74 +29,94 @@
     return lax.rem(lax.axis_index("energy"), 2)
 
 
-def embed(ref, rows, columns, real, imag):
-    high = ref.shape[0] // 2
-    wide = ref.shape[1] // 2
-    (r0, r1), (c0, c1) = rows, columns
-    ref[r0:r1, c0:c1] = real
-    ref[high + r0 : high + r1, c0:c1] = imag
-    ref[r0:r1, wide + c0 : wide + c1] = -imag
-    ref[high + r0 : high + r1, wide + c0 : wide + c1] = real
+def place(ref, column_half, value):
+    half = value.shape[1]
+    start = column_half * 2 * half
+    ref[:, start : start + half] = value
+    for row in range(0, value.shape[0], 2 * half):
+        ref[row : row + half, start + half : start + 2 * half] = -value[row + half : row + 2 * half]
+        ref[row + half : row + 2 * half, start + half : start + 2 * half] = value[row : row + half]
+
+
+def column_of(matrix, column_half):
+    half = matrix.shape[1] // 4
+    return matrix[:, column_half * 2 * half : column_half * 2 * half + half]
 
 
 def prepare(row_ref, coupling_ref, states_ref, forward_ref, backward_ref, drive_ref, sums):
     order = coupling_ref.shape[-1]
-    whole = ((0, order), (0, order))
-    real, imag = coupling_ref[0], coupling_ref[1]
-    embed(forward_ref, *whole, real, imag)
-    embed(backward_ref, *whole, real.T, -imag.T)
+    half = order // 2
     sums[...] = jnp.zeros_like(sums)
-    for contact in range(states_ref.shape[0]):
+
+    @pl.loop(0, states_ref.shape[0])
+    def _(contact):
         row = row_ref[contact]
         sums[row] = sums[row] + states_ref[contact].astype(jnp.float32)
-    drive = sums[...].astype(jnp.bfloat16)
-    block_rows, _, count, _ = drive.shape
+
+    block_rows, _, count, _ = sums.shape
     count = block_rows * count
-    embed(
-        drive_ref,
-        (0, count),
-        (0, order),
-        drive[:, 0].reshape(count, order),
-        drive[:, 1].reshape(count, order),
-    )
+
+    def arrange(first):
+        def block(part, i, j):
+            rows, columns = ((first ^ k) * half for k in (i, j))
+            return coupling_ref[part, rows : rows + half, columns : columns + half]
+
+        for j in range(2):
+            ahead, back = [], []
+            for i in range(2):
+                ahead += [block(0, i, j), block(1, i, j)]
+                back += [block(0, j, i).T, -block(1, j, i).T]
+            place(forward_ref, j, jnp.concatenate(ahead, axis=0))
+            place(backward_ref, j, jnp.concatenate(back, axis=0))
+        for h in range(2):
+            left = h * half
+            right = order + left
+            start = (first ^ h) * half
+            real, imag = (
+                sums[:, part, :, start : start + half].astype(jnp.bfloat16).reshape(count, half)
+                for part in range(2)
+            )
+            drive_ref[:count, left : left + half] = real
+            drive_ref[count:, left : left + half] = imag
+            drive_ref[:count, right : right + half] = -imag
+            drive_ref[count:, right : right + half] = real
+
+    for first in range(2):
+        pl.when(row_bit() == first)(functools.partial(arrange, first))
 
 
 def assemble(step, fetched, green):
-    row, column = row_bit(), core_bit()
     own_ref, side_ref, cross_ref, down_ref = fetched
     half = own_ref.shape[-1]
-    for blocks, a, b in (
-        (own_ref, row, column),
-        (side_ref, row, 1 - column),
-        (cross_ref, 1 - row, 1 - column),
-        (down_ref, 1 - row, column),
-    ):
-        for part in range(2):
-            start = pl.multiple_of(part * 2 * half + a * half, half)
-            green[b, pl.ds(start, half), :] = blocks[step, part]
-
-
-def own_rows(matrix, part):
-    half = matrix.shape[0] // 4
-    start = pl.multiple_of(part * 2 * half + row_bit() * half, half)
-    return matrix[pl.ds(start, half), :]
+
+    def fill(mine):
+        for blocks, row, column in (
+            (own_ref, 0, mine),
+            (side_ref, 0, 1 - mine),
+            (cross_ref, 1, 1 - mine),
+            (down_ref, 1, mine),
+        ):
+            for part in range(2):
+                start = (2 * row + part) * half
+                green[column, start : start + half, :] = blocks[step, part]
+
+    for mine in range(2):
+        pl.when(lax.rem(row_bit() + core_bit(), 2) == mine)(functools.partial(fill, mine))
 
 
 def step_products(source, target, green, products, surface_from, surface):
     order = source[0].shape[0] // 2
     half = order // 2
     for coupling, product in zip(source, products):
-        for b in range(2):
-            value = dot(coupling[...], green[b]).astype(jnp.bfloat16)
-            embed(product, (0, order), (b * half, (b + 1) * half), value[:order], value[order:])
-    for part in range(2):
-        term = dot(own_rows(products[0], part), source[1][:, :order])
-        surface[part] = term if surface_from is None else surface_from[part] + term
+        for h in range(2):
+            place(product, h, dot(coupling[...], green[h]).astype(jnp.bfloat16))
+    for h in range(2):
+        term = dot(products[0][:order, :], column_of(source[1], h))
+        columns = slice(h * half, (h + 1) * half)
+        surface[:, columns] = term if surface_from is None else surface_from[:, columns] + term
     for product, coupling, following in zip(products, source, target):
-        for b in range(2):
-            columns = (b * half, (b + 1) * half)
-            value = dot(product[...], coupling[:, columns[0] : columns[1]]).astype(jnp.bfloat16)
-            embed(following, (0, order), columns, value[:order], value[order:])
+        for h in range(2):
+            place(following, h, dot(product[...], column_of(coupling, h)).astype(jnp.bfloat16))
 
 
 def first_steps(
@@ -133,19 +155,16 @@
     copies[2].start()
     order = forward.shape[0] // 2
     half = order // 2
-    for b in range(2):
-        columns = (b * half, (b + 1) * half)
-        real = dot(own_rows(forward, 0), green[b]).astype(jnp.bfloat16)
-        imag = dot(own_rows(forward, 1), green[b]).astype(jnp.bfloat16)
-        embed(forward_rows, (0, half), columns, real, imag)
+    for h in range(2):
+        place(forward_rows, h, dot(forward[:order, :], green[h]).astype(jnp.bfloat16))
     copies[3].start()
     energy = []
-    for part in range(2):
-        rows = forward_rows[part * half : (part + 1) * half, :]
-        energy.append((surface[part] + dot(rows, backward[:, :order])).astype(jnp.bfloat16))
+    for h in range(2):
+        term = dot(forward_rows[...], column_of(backward, h))
+        energy.append((surface[:, h * half : (h + 1) * half] + term).astype(jnp.bfloat16))
     value = lax.dot_general(
         drive_ref[...],
-        jnp.concatenate(energy, axis=1),
+        jnp.concatenate([e[part * half : (part + 1) * half] for part in range(2) for e in energy], axis=1),
         (((1,), (1,)), ((), ())),
         preferred_element_type=jnp.float32,
     ).astype(jnp.bfloat16)
@@ -157,30 +176,46 @@
         copy.wait()
 
 
-def far_blocks(forward, backward, green, forward_rows, kept_ref, given_ref, backward_rows):
+def far_blocks(
+    forward_in, backward_in, green_in, forward_rows_in, kept_ref, given_ref,
+    forward, backward, green, forward_rows, backward_rows, copy_sems,
+):
+    arriving = (backward_in, green_in, forward_rows_in, forward_in)
+    held = (backward, green, forward_rows, forward)
+    copies = [
+        pltpu.make_async_copy(source, kept, copy_sems.at[i])
+        for i, (source, kept) in enumerate(zip(arriving, held))
+    ]
+    for copy in copies:
+        copy.start()
     order = forward.shape[0] // 2
     half = order // 2
-    core = core_bit()
-    for b in range(2):
-        columns = (b * half, (b + 1) * half)
-        real = dot(own_rows(backward, 0), green[b]).astype(jnp.bfloat16)
-        imag = dot(own_rows(backward, 1), green[b]).astype(jnp.bfloat16)
-        embed(backward_rows, (0, half), columns, real, imag)
+    mine = lax.rem(row_bit() + core_bit(), 2)
+    copies[0].wait()
+    copies[1].wait()
+    for h in range(2):
+        place(backward_rows, h, dot(backward[:order, :], green[h]).astype(jnp.bfloat16))
+    copies[2].wait()
+    copies[3].wait()
     for which, rows, coupling in ((0, forward_rows, forward), (1, backward_rows, backward)):
-        for b in range(2):
-            for part in range(2):
-                value = dot(
-                    rows[part * half : (part + 1) * half, :],
-                    coupling[:, b * half : (b + 1) * half],
-                ).astype(jnp.bfloat16)
-
-                @pl.when(core == b)
-                def _():
-                    kept_ref[which, part] = value
-
-                @pl.when(core != b)
-                def _():
-                    given_ref[which, part] = value
+        for h in range(2):
+            value = dot(rows[...], column_of(coupling, h)).astype(jnp.bfloat16)
+
+            @pl.when(mine == h)
+            def _():
+                kept_ref[which, 0] = value[:half]
+                kept_ref[which, 1] = value[half:]
+
+            @pl.when(mine != h)
+            def _():
+                given_ref[which, 0] = value[:half]
+                given_ref[which, 1] = value[half:]
+
+
+def choose(kept_ref, given_ref, forward_ref, backward_ref):
+    worker = lax.rem(lax.axis_index("rows"), 2) == core_bit()
+    for which, far_ref in enumerate((forward_ref, backward_ref)):
+        far_ref[0] = jnp.where(worker, kept_ref[which], given_ref[which])
 
 
 def spread(assignment_ref, weight_ref, received_ref, injection_ref, weighted_ref):
@@ -200,9 +235,14 @@
                 weighted_ref[copy, part, :, a * half : (a + 1) * half] = total
 
 
-def call(body, outs, scratch, scalars=0, vmem=32, far_outs=0):
+def in_hbm(*arrays):
+    return [pltpu.with_memory_space_constraint(array, pltpu.HBM) for array in arrays]
+
+
+def call(body, outs, scratch, scalars=0, vmem=32, far_outs=0, far_ins=0):
     def run(*operands):
         specs = [SMEM_WHOLE] * scalars + [VMEM_WHOLE] * (len(operands) - scalars)
+        specs[:far_ins] = [HBM_WHOLE] * far_ins
         return pl.pallas_call(
             body,
             out_shape=outs,
@@ -251,7 +291,8 @@
 
     square_scratch = pltpu.VMEM((2 * order, 2 * order), bf16)
     green_shape = (2, 2 * order, half)
-    surface_shape = (2, half, order)
+    surface_shape = (order, order)
+    rows_scratch = pltpu.VMEM((order, 2 * order), bf16)
     forward, backward, surface = call(
         first_steps,
         (square, square, jax.ShapeDtypeStruct(surface_shape, f32)),
@@ -270,7 +311,7 @@
             square_scratch,
             square_scratch,
             pltpu.VMEM(green_shape, bf16),
-            pltpu.VMEM((order, 2 * order), bf16),
+            rows_scratch,
             pltpu.VMEM(surface_shape, f32),
             square_scratch,
             square_scratch,
@@ -283,11 +324,21 @@
 
     far_shape = jax.ShapeDtypeStruct((2, 2, half, half), bf16)
     kept, given = call(
-        far_blocks, (far_shape, far_shape), [pltpu.VMEM((order, 2 * order), bf16)]
-    )(forward, backward, green, forward_rows)
+        far_blocks,
+        (far_shape, far_shape),
+        [
+            square_scratch,
+            square_scratch,
+            pltpu.VMEM(green_shape, bf16),
+            rows_scratch,
+            rows_scratch,
+            pltpu.SemaphoreType.DMA((4,)),
+        ],
+        far_ins=4,
+    )(*in_hbm(forward, backward, green, forward_rows))
     given = lax.ppermute(given, both, routes(1, False))
-    worker = lax.axis_index("rows") % 2 == core_bit()
-    far_out = jnp.where(worker, kept, given)
+    block_shape = jax.ShapeDtypeStruct((1, 2, half, half), bf16)
+    far_forward, far_backward = call(choose, (block_shape, block_shape), [])(kept, given)
 
     groups = assignment.shape[0]
     chips = energies_axis // 2
@@ -309,7 +360,7 @@
         part_sum.astype(bf16), "energy", [(i, i ^ 1) for i in range(energies_axis)]
     )
     integrated = part_sum + other_sum.astype(f32)
-    return injection[:, None], integrated[None], far_out[0][None], far_out[1][None]
+    return injection[:, None], integrated[None], far_forward, far_backward
 
 
 def solution(mesh):

time: 98.7 us -> 101 us (1.023)
  the two profiles are of different devices: /device:TPU:1 before, /device:TPU:2 now
where the time goes in v2:
time: 101 us; the launch traced here: 100 us
  starting transfers between devices  39.5 us (39%)
  Pallas kernels  28.6 us (28%)
  blocking collectives  20 us (20%)
  waiting for transfers between devices  7.81 us (8%)
  local copies, waits for them, and re-layouts  2.63 us (3%)
    pallas_call x6, Pallas kernels, run(): pl.pallas_call(body, out_shape=outs, in_specs=specs, out_specs=tuple((HBM...  28.6 us
    ppermute x6, starting transfers between devices, local(): fetched[c].append(lax.ppermute(chunk, both, routes(flip, True)))  26 us
    all_to_all x1, blocking collectives, local(): lax.all_to_all(injected, 'rows', split_axis=0, concat_axis=0, tiled=True)  20 us
    all_to_all x1, starting transfers between devices, local(): lax.all_to_all(weighted, 'energy', split_axis=0, concat_axis=0, axis_inde...  10.3 us
    ppermute x1, waiting for transfers between devices, local(): given = lax.ppermute(given, both, routes(1, False))  4.35 us
    all_to_all x1, waiting for transfers between devices, local(): lax.all_to_all(weighted, 'energy', split_axis=0, concat_axis=0, axis_inde...  3.44 us
  transfers between devices with their start and end apart: 9, of which 2 were waited for; matrix products, arithmetic and copies ran while one was open for 0% of the time, Pallas kernels for 19%

profile of v2, /device:TPU:2, one launch (start us, length us, event | category | flops | bytes accessed | tf_op | source)
XLA Modules:
  0.0 100.1 jit_solution(939634693399381964)
XLA Ops:
  0.7 1.4 %slice_bitcast_fusion = (bf16[2,2,256,256]{3,2,1,0:T(8,128)(2,1)S(1)}, bf16[2,2,256,256]{3,2,1,0:T(8,128)(2,1)S(1)}) fusion(bf16[1,4,2,256,256]{4,3,2,1,0:T(8,128)(2,1)} %param.7), kind=kLoop, calls=%fused_computation.1 | loop fusion | bytes 2097152 | tf_op jit(solution)/shard_map/squeeze | solution.py:275
  2.0 0.7 collective-permute-start.2
  2.7 10.5 %collective-permute-start.1 = (bf16[2,2,256,256]{3,2,1,0:T(8,128)(2,1)S(1)}, bf16[2,2,256,256]{3,2,1,0:T(8,128)(2,1)S(1)}, u32[]{:S(2)}, u32[]{:S(2)}) collective-permute-start(bf16[2,2,256,256]{3,2,1,0:T(8,128)(2,1)S(1)} %get-tuple-element.43.own_ref), channel_id=1, source_target_pairs={{3,0},{1,2},{7,4},{5,6},{11,8},{9,10},{15,12},{13,14},{19,16},{17,... | collective-permute-start | bytes 1572872 | tf_op jit(solution)/shard_map/ppermute | solution.py:280
  13.2 1.3 %collective-permute-start = (bf16[2,2,256,256]{3,2,1,0:T(8,128)(2,1)S(1)}, bf16[2,2,256,256]{3,2,1,0:T(8,128)(2,1)S(1)}, u32[]{:S(2)}, u32[]{:S(2)}) collective-permute-start(bf16[2,2,256,256]{3,2,1,0:T(8,128)(2,1)S(1)} %get-tuple-element.43.own_ref), channel_id=1, source_target_pairs={{1,0},{3,2},{5,4},{7,6},{9,8},{11,10},{13,12},{15,14},{17,16},{19,... | collective-permute-start | bytes 1572872 | tf_op jit(solution)/shard_map/ppermute | solution.py:280
  14.6 0.7 collective-permute-start.5
  15.3 2.5 %collective-permute-start.4 = (bf16[2,2,256,256]{3,2,1,0:T(8,128)(2,1)S(1)}, bf16[2,2,256,256]{3,2,1,0:T(8,128)(2,1)S(1)}, u32[]{:S(2)}, u32[]{:S(2)}) collective-permute-start(bf16[2,2,256,256]{3,2,1,0:T(8,128)(2,1)S(1)} %get-tuple-element.42.own_ref), channel_id=1, source_target_pairs={{3,0},{1,2},{7,4},{5,6},{11,8},{9,10},{15,12},{13,14},{19,16},{17,... | collective-permute-start | bytes 1572872 | tf_op jit(solution)/shard_map/ppermute | solution.py:280
  17.8 0.0 collective-permute-done.2.down_ref
  17.8 10.3 %collective-permute-start.3 = (bf16[2,2,256,256]{3,2,1,0:T(8,128)(2,1)S(1)}, bf16[2,2,256,256]{3,2,1,0:T(8,128)(2,1)S(1)}, u32[]{:S(2)}, u32[]{:S(2)}) collective-permute-start(bf16[2,2,256,256]{3,2,1,0:T(8,128)(2,1)S(1)} %get-tuple-element.42.own_ref), channel_id=1, source_target_pairs={{1,0},{3,2},{5,4},{7,6},{9,8},{11,10},{13,12},{15,14},{17,16},{19,... | collective-permute-start | bytes 1572872 | tf_op jit(solution)/shard_map/ppermute | solution.py:280
  28.1 0.0 copy-start.1
  28.1 1.2 %copy-done.1 = bf16[2,512,512]{2,1,0:T(8,128)(2,1)S(1)} copy-done((bf16[2,512,512]{2,1,0:T(8,128)(2,1)S(1)}, bf16[2,512,512]{2,1,0:T(8,128)(2,1)}, u32[]{:S(2)}) %copy-start.1) | copy-done | bytes 1048600
  29.3 1.9 %shard_map.93 = (bf16[1024,1024]{1,0:T(8,128)(2,1)S(1)}, bf16[1024,1024]{1,0:T(8,128)(2,1)S(1)}, bf16[1024,1024]{1,0:T(8,128)(2,1)S(1)}) custom-call(s32[48]{0:T(128)S(1)} %copy-done.4, bf16[2,512,512]{2,1,0:T(8,128)(2,1)S(1)} %copy-done.1, bf16[48,2,16,512]{3,2,1,0:T(8,128)(2,1)S(1)} %copy-done), custom_call_target="tpu_custom_call" | custom-call | tf_op jit(solution)/shard_map/pallas_call | solution.py:246
  31.2 0.0 collective-permute-done.1.cross_ref
  31.2 0.0 collective-permute-done.side_ref
  31.3 10.2 %shard_map.94 = (bf16[1024,1024]{1,0:T(8,128)(2,1)S(1)}, bf16[1024,1024]{1,0:T(8,128)(2,1)S(1)}, f32[512,512]{1,0:T(8,128)S(1)}) custom-call(bf16[1024,1024]{1,0:T(8,128)(2,1)S(1)} %get-tuple-element.21.forward_in, bf16[1024,1024]{1,0:T(8,128)(2,1)S(1)} %get-tuple-element.22.backward_in, bf16[2,2,256,256]{3,2,1,0:T(8,128)(2,1)S(1)} %get-tuple-element.43.own_ref, ...), custom_call_target="tpu_custom_call" | custom-call | tf_op jit(solution)/shard_map/pallas_call | solution.py:246
  41.5 0.0 collective-permute-done.5.down_ref
  41.5 0.0 collective-permute-done.4.cross_ref
  41.5 0.0 collective-permute-done.3.side_ref
  41.5 0.0 copy-start.2
  41.5 0.0 copy-start.3
  41.6 8.4 %shard_map.95 = (bf16[1024,1024]{1,0:T(8,128)(2,1)}, bf16[1024,1024]{1,0:T(8,128)(2,1)}, bf16[2,1024,256]{2,1,0:T(8,128)(2,1)}, bf16[512,1024]{1,0:T(8,128)(2,1)}, bf16[32,2,16,256]{3,2,1,0:T(8,128)(2,1)S(1)}) custom-call(bf16[1024,1024]{1,0:T(8,128)(2,1)S(1)} %get-tuple-element.23.forward_in, bf16[1024,1024]{1,0:T(8,128)(2,1)S(1)} %get-tuple-element.24.backward_in, ...), custom_call_target="tpu_custom_call" | custom-call | tf_op jit(solution)/shard_map/pallas_call | solution.py:246
  49.9 20.0 %all_to_all.10 = bf16[32,2,16,256]{3,2,1,0:T(8,128)(2,1)S(1)} all-to-all(bf16[32,2,16,256]{3,2,1,0:T(8,128)(2,1)S(1)} %get-tuple-element.27), channel_id=1, replica_groups=mesh['energy'=16,'rows'=32] {'rows'}, dimensions={0} | all-to-all | bytes 1048576 | tf_op jit(solution)/shard_map/all_to_all | solution.py:323
  70.0 0.0 copy-done.2
  70.0 1.5 %shard_map.96 = (f32[8,2,16,512]{3,2,1,0:T(8,128)}, bf16[8,2,16,512]{3,2,1,0:T(8,128)(2,1)}) custom-call(s32[8]{0:T(128)S(1)} %copy-done.2, f32[8]{0:T(128)S(1)} %copy-done.3, bf16[8,2,2,2,16,256]{5,4,3,2,1,0:T(8,128)(2,1)S(1)} %bitcast.10), custom_call_target="tpu_custom_call" | custom-call | tf_op jit(solution)/shard_map/pallas_call | solution.py:246
  71.5 10.3 %all-to-all-start.1 = ((bf16[8,2,16,512]{3,2,1,0:T(8,128)(2,1)}), bf16[8,2,16,512]{3,2,1,0:T(8,128)(2,1)S(1)}, u32[]{:S(2)}, u32[]{:S(2)}) async-start(bf16[8,2,16,512]{3,2,1,0:T(8,128)(2,1)} %get-tuple-element.29), calls=%async_computation.1 | async-start | bytes 524288 | tf_op jit(solution)/shard_map/all_to_all | solution.py:355
  81.8 5.7 %shard_map.97 = (bf16[2,2,256,256]{3,2,1,0:T(8,128)(2,1)S(1)}, bf16[2,2,256,256]{3,2,1,0:T(8,128)(2,1)S(1)}) custom-call(bf16[1024,1024]{1,0:T(8,128)(2,1)} %get-tuple-element.30.forward_in, bf16[1024,1024]{1,0:T(8,128)(2,1)} %get-tuple-element.31.backward_in, bf16[2,1024,256]{2,1,0:T(8,128)(2,1)} %get-tuple-element.32.green_in, ...), custom_call_target="tpu_custom_call" | custom-call | tf_op jit(solution)/shard_map/pallas_call | solution.py:246
  87.5 1.3 %collective-permute-start.7 = (bf16[2,2,256,256]{3,2,1,0:T(8,128)(2,1)S(1)}, bf16[2,2,256,256]{3,2,1,0:T(8,128)(2,1)S(1)}, u32[]{:S(2)}, u32[]{:S(2)}) collective-permute-start(bf16[2,2,256,256]{3,2,1,0:T(8,128)(2,1)S(1)} %get-tuple-element.35), channel_id=1, source_target_pairs={{0,1},{2,3},{4,5},{6,7},{8,9},{10,11},{12,13},{14,15},{16,17},{18,... | collective-permute-start | bytes 1572872 | tf_op jit(solution)/shard_map/ppermute | solution.py:339
  88.8 3.4 %all-to-all-done.1 = bf16[8,2,16,512]{3,2,1,0:T(8,128)(2,1)S(1)} async-done(((bf16[8,2,16,512]{3,2,1,0:T(8,128)(2,1)}), bf16[8,2,16,512]{3,2,1,0:T(8,128)(2,1)S(1)}, u32[]{:S(2)}, u32[]{:S(2)}) %all-to-all-start.1) | async-done | bytes 262176 | tf_op jit(solution)/shard_map/all_to_all | solution.py:355
  92.3 1.9 %collective-permute-start.6 = (bf16[2,16,512]{2,1,0:T(8,128)(2,1)S(1)}, bf16[2,16,512]{2,1,0:T(8,128)(2,1)S(1)}, u32[]{:S(2)}, u32[]{:S(2)}) collective-permute-start(bf16[2,16,512]{2,1,0:T(8,128)(2,1)S(1)} %convert_element_type.10), channel_id=1, source_target_pairs={{0,32},{32,0},{64,96},{96,64},{128,160},{160,128},{192,224},{224,1... | collective-permute-start | bytes 98312 | tf_op jit(solution)/shard_map/ppermute | solution.py:359
  94.2 4.3 %collective-permute-done.7.given_ref = bf16[2,2,256,256]{3,2,1,0:T(8,128)(2,1)S(1)} collective-permute-done((bf16[2,2,256,256]{3,2,1,0:T(8,128)(2,1)S(1)}, bf16[2,2,256,256]{3,2,1,0:T(8,128)(2,1)S(1)}, u32[]{:S(2)}, u32[]{:S(2)}) %collective-permute-start.7) | collective-permute-done | bytes 524320 | tf_op jit(solution)/shard_map/ppermute | solution.py:339
  98.6 0.8 shard_map.98
  99.4 0.0 collective-permute-done.6
  99.4 0.6 add_bitcast_fusion
  (7 shorter events, 0.1 us)
Async XLA Ops:
  0.6 27.4 %copy-start = (bf16[48,2,16,512]{3,2,1,0:T(8,128)(2,1)S(1)}, bf16[48,2,16,512]{3,2,1,0:T(8,128)(2,1)}, u32[]{:S(2)}) copy-start(bf16[48,2,16,512]{3,2,1,0:T(8,128)(2,1)} %states_ref.1) | copy-start | bytes 4718596
  0.6 27.4 %copy-start.4 = (s32[48]{0:T(128)S(1)}, s32[48]{0:T(128)}, u32[]{:S(2)}) copy-start(s32[48]{0:T(128)} %row_ref.1) | copy-start | bytes 580
  2.0 15.7 %collective-permute-start.2 = (bf16[2,2,256,256]{3,2,1,0:T(8,128)(2,1)S(1)}, bf16[2,2,256,256]{3,2,1,0:T(8,128)(2,1)S(1)}, u32[]{:S(2)}, u32[]{:S(2)}) collective-permute-start(bf16[2,2,256,256]{3,2,1,0:T(8,128)(2,1)S(1)} %get-tuple-element.43.own_ref), channel_id=1, source_target_pairs={{2,0},{0,2},{6,4},{4,6},{10,8},{8,10},{14,12},{12,14},{18,16},{16,... | collective-permute-start | bytes 1572872 | tf_op jit(solution)/shard_map/ppermute | solution.py:280
  2.7 28.5 %collective-permute-start.1 = (bf16[2,2,256,256]{3,2,1,0:T(8,128)(2,1)S(1)}, bf16[2,2,256,256]{3,2,1,0:T(8,128)(2,1)S(1)}, u32[]{:S(2)}, u32[]{:S(2)}) collective-permute-start(bf16[2,2,256,256]{3,2,1,0:T(8,128)(2,1)S(1)} %get-tuple-element.43.own_ref), channel_id=1, source_target_pairs={{3,0},{1,2},{7,4},{5,6},{11,8},{9,10},{15,12},{13,14},{19,16},{17,... | collective-permute-start | bytes 1572872 | tf_op jit(solution)/shard_map/ppermute | solution.py:280
  13.2 18.0 %collective-permute-start = (bf16[2,2,256,256]{3,2,1,0:T(8,128)(2,1)S(1)}, bf16[2,2,256,256]{3,2,1,0:T(8,128)(2,1)S(1)}, u32[]{:S(2)}, u32[]{:S(2)}) collective-permute-start(bf16[2,2,256,256]{3,2,1,0:T(8,128)(2,1)S(1)} %get-tuple-element.43.own_ref), channel_id=1, source_target_pairs={{1,0},{3,2},{5,4},{7,6},{9,8},{11,10},{13,12},{15,14},{17,16},{19,... | collective-permute-start | bytes 1572872 | tf_op jit(solution)/shard_map/ppermute | solution.py:280
  14.6 26.9 %collective-permute-start.5 = (bf16[2,2,256,256]{3,2,1,0:T(8,128)(2,1)S(1)}, bf16[2,2,256,256]{3,2,1,0:T(8,128)(2,1)S(1)}, u32[]{:S(2)}, u32[]{:S(2)}) collective-permute-start(bf16[2,2,256,256]{3,2,1,0:T(8,128)(2,1)S(1)} %get-tuple-element.42.own_ref), channel_id=1, source_target_pairs={{2,0},{0,2},{6,4},{4,6},{10,8},{8,10},{14,12},{12,14},{18,16},{16,... | collective-permute-start | bytes 1572872 | tf_op jit(solution)/shard_map/ppermute | solution.py:280
  15.3 26.2 %collective-permute-start.4 = (bf16[2,2,256,256]{3,2,1,0:T(8,128)(2,1)S(1)}, bf16[2,2,256,256]{3,2,1,0:T(8,128)(2,1)S(1)}, u32[]{:S(2)}, u32[]{:S(2)}) collective-permute-start(bf16[2,2,256,256]{3,2,1,0:T(8,128)(2,1)S(1)} %get-tuple-element.42.own_ref), channel_id=1, source_target_pairs={{3,0},{1,2},{7,4},{5,6},{11,8},{9,10},{15,12},{13,14},{19,16},{17,... | collective-permute-start | bytes 1572872 | tf_op jit(solution)/shard_map/ppermute | solution.py:280
  17.8 23.7 %collective-permute-start.3 = (bf16[2,2,256,256]{3,2,1,0:T(8,128)(2,1)S(1)}, bf16[2,2,256,256]{3,2,1,0:T(8,128)(2,1)S(1)}, u32[]{:S(2)}, u32[]{:S(2)}) collective-permute-start(bf16[2,2,256,256]{3,2,1,0:T(8,128)(2,1)S(1)} %get-tuple-element.42.own_ref), channel_id=1, source_target_pairs={{1,0},{3,2},{5,4},{7,6},{9,8},{11,10},{13,12},{15,14},{17,16},{19,... | collective-permute-start | bytes 1572872 | tf_op jit(solution)/shard_map/ppermute | solution.py:280
  28.1 1.2 %copy-start.1 = (bf16[2,512,512]{2,1,0:T(8,128)(2,1)S(1)}, bf16[2,512,512]{2,1,0:T(8,128)(2,1)}, u32[]{:S(2)}) copy-start(bf16[2,512,512]{2,1,0:T(8,128)(2,1)} %coupling_ref.1) | copy-start | bytes 3145732
  41.5 28.4 %copy-start.2 = (s32[8]{0:T(128)S(1)}, s32[8]{0:T(128)}, u32[]{:S(2)}) copy-start(s32[8]{0:T(128)} %assignment_ref.1) | copy-start | bytes 100
  41.5 28.4 %copy-start.3 = (f32[8]{0:T(128)S(1)}, f32[8]{0:T(128)}, u32[]{:S(2)}) copy-start(f32[8]{0:T(128)} %weight_ref.1) | copy-start | bytes 100
  71.5 20.8 %all-to-all-start.1 = ((bf16[8,2,16,512]{3,2,1,0:T(8,128)(2,1)}), bf16[8,2,16,512]{3,2,1,0:T(8,128)(2,1)S(1)}, u32[]{:S(2)}, u32[]{:S(2)}) async-start(bf16[8,2,16,512]{3,2,1,0:T(8,128)(2,1)} %get-tuple-element.29), calls=%async_computation.1 | async-start | bytes 524288 | tf_op jit(solution)/shard_map/all_to_all | solution.py:355
  87.5 11.1 %collective-permute-start.7 = (bf16[2,2,256,256]{3,2,1,0:T(8,128)(2,1)S(1)}, bf16[2,2,256,256]{3,2,1,0:T(8,128)(2,1)S(1)}, u32[]{:S(2)}, u32[]{:S(2)}) collective-permute-start(bf16[2,2,256,256]{3,2,1,0:T(8,128)(2,1)S(1)} %get-tuple-element.35), channel_id=1, source_target_pairs={{0,1},{2,3},{4,5},{6,7},{8,9},{10,11},{12,13},{14,15},{16,17},{18,... | collective-permute-start | bytes 1572872 | tf_op jit(solution)/shard_map/ppermute | solution.py:339
  92.3 7.1 %collective-permute-start.6 = (bf16[2,16,512]{2,1,0:T(8,128)(2,1)S(1)}, bf16[2,16,512]{2,1,0:T(8,128)(2,1)S(1)}, u32[]{:S(2)}, u32[]{:S(2)}) collective-permute-start(bf16[2,16,512]{2,1,0:T(8,128)(2,1)S(1)} %convert_element_type.10), channel_id=1, source_target_pairs={{0,32},{32,0},{64,96},{96,64},{128,160},{160,128},{192,224},{224,1... | collective-permute-start | bytes 98312 | tf_op jit(solution)/shard_map/ppermute | solution.py:359

commit v3 on v2

--- a/solution.py
+++ b/solution.py
@@ -230,9 +230,7 @@
                 value = received_ref[slot, a, column, part].astype(jnp.float32)
                 injection_ref[e, part, :, a * half : (a + 1) * half] = value
                 total = total + weight_ref[e] * value
-            total = total.astype(weighted_ref.dtype)
-            for copy in range(weighted_ref.shape[0]):
-                weighted_ref[copy, part, :, a * half : (a + 1) * half] = total
+            weighted_ref[part, :, a * half : (a + 1) * half] = total.astype(weighted_ref.dtype)
 
 
 def in_hbm(*arrays):
@@ -253,6 +251,27 @@
         )(*operands)
 
     return run
+
+
+def over_energies(energies_axis, own):
+    chips = energies_axis // 2
+    assert chips == 8
+
+    def from_chip(value, distance):
+        pairs = [
+            ((chip + distance) % chips * 2 + core, chip * 2 + core)
+            for chip in range(chips)
+            for core in range(2)
+        ]
+        return lax.ppermute(value, "energy", pairs)
+
+    after = from_chip(own, 1)
+    before = from_chip(own, -1)
+    two = own.astype(jnp.float32) + after.astype(jnp.float32)
+    three = two + before.astype(jnp.float32)
+    ahead = from_chip(three.astype(own.dtype), 3)
+    behind = from_chip(two.astype(own.dtype), -3)
+    return three + ahead.astype(jnp.float32) + behind.astype(jnp.float32)
 
 
 def local(energies_axis, rows_axis, coupling, inverses, contact_row, assignment, states, weights):
@@ -341,25 +360,18 @@
     far_forward, far_backward = call(choose, (block_shape, block_shape), [])(kept, given)
 
     groups = assignment.shape[0]
-    chips = energies_axis // 2
     injection, weighted = call(
         spread,
         (
             jax.ShapeDtypeStruct((groups, 2, count, order), f32),
-            jax.ShapeDtypeStruct((chips, 2, count, order), bf16),
+            jax.ShapeDtypeStruct((2, count, order), bf16),
         ),
         [],
         scalars=2,
     )(assignment, weights, received.reshape(slots, 2, 2, 2, count, half))
-    alike = [[2 * chip + core for chip in range(chips)] for core in range(2)]
-    gathered = lax.all_to_all(
-        weighted, "energy", split_axis=0, concat_axis=0, axis_index_groups=alike, tiled=True
-    )
-    part_sum = jnp.sum(gathered.astype(f32), axis=0)
-    other_sum = lax.ppermute(
-        part_sum.astype(bf16), "energy", [(i, i ^ 1) for i in range(energies_axis)]
-    )
-    integrated = part_sum + other_sum.astype(f32)
+    total = over_energies(energies_axis, weighted)
+    other = lax.ppermute(total.astype(bf16), "energy", [(i, i ^ 1) for i in range(energies_axis)])
+    integrated = total + other.astype(f32)
     return injection[:, None], integrated[None], far_forward, far_backward
 
 

time: 101 us -> 112 us (1.11)
  the two profiles are of different devices: /device:TPU:2 before, /device:TPU:1 now
where the time goes in v3:
time: 112 us
  starting transfers between devices  45.1 us (40%)
  Pallas kernels  28.5 us (25%)
  blocking collectives  25.8 us (23%)
  waiting for transfers between devices  7.99 us (7%)
  local copies, waits for them, and re-layouts  2.63 us (2%)
    pallas_call x6, Pallas kernels, run(): pl.pallas_call(body, out_shape=outs, in_specs=specs, out_specs=tuple((HBM...  28.5 us
    all_to_all x1, blocking collectives, local(): lax.all_to_all(injected, 'rows', split_axis=0, concat_axis=0, tiled=True)  25.8 us
    ppermute x4, starting transfers between devices, from_chip(): return lax.ppermute(value, 'energy', pairs)  19.7 us
    ppermute x6, starting transfers between devices, local(): fetched[c].append(lax.ppermute(chunk, both, routes(flip, True)))  15.9 us
    ppermute x1, starting transfers between devices, local(): lax.ppermute(total.astype(bf16), 'energy', [(i, i ^ 1) for i in range(ene...  8.14 us
    ppermute x4, waiting for transfers between devices, from_chip(): return lax.ppermute(value, 'energy', pairs)  4.3 us
    ppermute x6, waiting for transfers between devices, local(): fetched[c].append(lax.ppermute(chunk, both, routes(flip, True)))  3.69 us
  transfers between devices with their start and end apart: 12, of which 2 were waited for; matrix products, arithmetic and copies ran while one was open for 0% of the time, Pallas kernels for 17%

profile of v3, /device:TPU:1, one launch (start us, length us, event | category | flops | bytes accessed | tf_op | source)
XLA Modules:
  0.0 111.6 jit_solution(16987754571959135333)
XLA Ops:
  0.7 1.4 %slice_bitcast_fusion = (bf16[2,2,256,256]{3,2,1,0:T(8,128)(2,1)S(1)}, bf16[2,2,256,256]{3,2,1,0:T(8,128)(2,1)S(1)}) fusion(bf16[1,4,2,256,256]{4,3,2,1,0:T(8,128)(2,1)} %param.7), kind=kLoop, calls=%fused_computation | loop fusion | bytes 2097152 | tf_op jit(solution)/shard_map/squeeze | solution.py:294
  2.0 0.7 collective-permute-start.2
  2.7 7.6 %collective-permute-start.1 = (bf16[2,2,256,256]{3,2,1,0:T(8,128)(2,1)S(1)}, bf16[2,2,256,256]{3,2,1,0:T(8,128)(2,1)S(1)}, u32[]{:S(2)}, u32[]{:S(2)}) collective-permute-start(bf16[2,2,256,256]{3,2,1,0:T(8,128)(2,1)S(1)} %get-tuple-element.43.own_ref), channel_id=1, source_target_pairs={{3,0},{1,2},{7,4},{5,6},{11,8},{9,10},{15,12},{13,14},{19,16},{17,... | collective-permute-start | bytes 1572872 | tf_op jit(solution)/shard_map/ppermute | solution.py:299
  10.3 1.3 %collective-permute-start = (bf16[2,2,256,256]{3,2,1,0:T(8,128)(2,1)S(1)}, bf16[2,2,256,256]{3,2,1,0:T(8,128)(2,1)S(1)}, u32[]{:S(2)}, u32[]{:S(2)}) collective-permute-start(bf16[2,2,256,256]{3,2,1,0:T(8,128)(2,1)S(1)} %get-tuple-element.43.own_ref), channel_id=1, source_target_pairs={{1,0},{3,2},{5,4},{7,6},{9,8},{11,10},{13,12},{15,14},{17,16},{19,... | collective-permute-start | bytes 1572872 | tf_op jit(solution)/shard_map/ppermute | solution.py:299
  11.7 0.7 collective-permute-start.5
  12.4 4.3 %collective-permute-start.4 = (bf16[2,2,256,256]{3,2,1,0:T(8,128)(2,1)S(1)}, bf16[2,2,256,256]{3,2,1,0:T(8,128)(2,1)S(1)}, u32[]{:S(2)}, u32[]{:S(2)}) collective-permute-start(bf16[2,2,256,256]{3,2,1,0:T(8,128)(2,1)S(1)} %get-tuple-element.42.own_ref), channel_id=1, source_target_pairs={{3,0},{1,2},{7,4},{5,6},{11,8},{9,10},{15,12},{13,14},{19,16},{17,... | collective-permute-start | bytes 1572872 | tf_op jit(solution)/shard_map/ppermute | solution.py:299
  16.7 1.3 %collective-permute-start.3 = (bf16[2,2,256,256]{3,2,1,0:T(8,128)(2,1)S(1)}, bf16[2,2,256,256]{3,2,1,0:T(8,128)(2,1)S(1)}, u32[]{:S(2)}, u32[]{:S(2)}) collective-permute-start(bf16[2,2,256,256]{3,2,1,0:T(8,128)(2,1)S(1)} %get-tuple-element.42.own_ref), channel_id=1, source_target_pairs={{1,0},{3,2},{5,4},{7,6},{9,8},{11,10},{13,12},{15,14},{17,16},{19,... | collective-permute-start | bytes 1572872 | tf_op jit(solution)/shard_map/ppermute | solution.py:299
  18.0 0.0 copy-start.1
  18.1 1.2 %copy-done.1 = bf16[2,512,512]{2,1,0:T(8,128)(2,1)S(1)} copy-done((bf16[2,512,512]{2,1,0:T(8,128)(2,1)S(1)}, bf16[2,512,512]{2,1,0:T(8,128)(2,1)}, u32[]{:S(2)}) %copy-start.1) | copy-done | bytes 1048600
  19.3 1.9 %shard_map.93 = (bf16[1024,1024]{1,0:T(8,128)(2,1)S(1)}, bf16[1024,1024]{1,0:T(8,128)(2,1)S(1)}, bf16[1024,1024]{1,0:T(8,128)(2,1)S(1)}) custom-call(s32[48]{0:T(128)S(1)} %copy-done.4, bf16[2,512,512]{2,1,0:T(8,128)(2,1)S(1)} %copy-done.1, bf16[48,2,16,512]{3,2,1,0:T(8,128)(2,1)S(1)} %copy-done), custom_call_target="tpu_custom_call" | custom-call | tf_op jit(solution)/shard_map/pallas_call | solution.py:244
  21.2 3.7 %collective-permute-done.1.cross_ref = bf16[2,2,256,256]{3,2,1,0:T(8,128)(2,1)S(1)} collective-permute-done((bf16[2,2,256,256]{3,2,1,0:T(8,128)(2,1)S(1)}, bf16[2,2,256,256]{3,2,1,0:T(8,128)(2,1)S(1)}, u32[]{:S(2)}, u32[]{:S(2)}) %collective-permute-start.1) | collective-permute-done | bytes 524320 | tf_op jit(solution)/shard_map/ppermute | solution.py:299
  24.9 0.0 collective-permute-done.side_ref
  24.9 10.2 %shard_map.94 = (bf16[1024,1024]{1,0:T(8,128)(2,1)S(1)}, bf16[1024,1024]{1,0:T(8,128)(2,1)S(1)}, f32[512,512]{1,0:T(8,128)S(1)}) custom-call(bf16[1024,1024]{1,0:T(8,128)(2,1)S(1)} %get-tuple-element.21.forward_in, bf16[1024,1024]{1,0:T(8,128)(2,1)S(1)} %get-tuple-element.22.backward_in, bf16[2,2,256,256]{3,2,1,0:T(8,128)(2,1)S(1)} %get-tuple-element.43.own_ref, ...), custom_call_target="tpu_custom_call" | custom-call | tf_op jit(solution)/shard_map/pallas_call | solution.py:244
  35.1 0.0 collective-permute-done.5.down_ref
  35.1 0.0 collective-permute-done.3.side_ref
  35.1 0.0 copy-start.2
  35.2 0.0 copy-start.3
  35.2 8.4 %shard_map.95 = (bf16[1024,1024]{1,0:T(8,128)(2,1)}, bf16[1024,1024]{1,0:T(8,128)(2,1)}, bf16[2,1024,256]{2,1,0:T(8,128)(2,1)}, bf16[512,1024]{1,0:T(8,128)(2,1)}, bf16[32,2,16,256]{3,2,1,0:T(8,128)(2,1)S(1)}) custom-call(bf16[1024,1024]{1,0:T(8,128)(2,1)S(1)} %get-tuple-element.23.forward_in, bf16[1024,1024]{1,0:T(8,128)(2,1)S(1)} %get-tuple-element.24.backward_in, ...), custom_call_target="tpu_custom_call" | custom-call | tf_op jit(solution)/shard_map/pallas_call | solution.py:244
  43.5 25.8 %all_to_all.5 = bf16[32,2,16,256]{3,2,1,0:T(8,128)(2,1)S(1)} all-to-all(bf16[32,2,16,256]{3,2,1,0:T(8,128)(2,1)S(1)} %get-tuple-element.27), channel_id=1, replica_groups=mesh['energy'=16,'rows'=32] {'rows'}, dimensions={0} | all-to-all | bytes 1048576 | tf_op jit(solution)/shard_map/all_to_all | solution.py:342
  69.3 1.4 %shard_map.96 = (f32[8,2,16,512]{3,2,1,0:T(8,128)}, bf16[2,16,512]{2,1,0:T(8,128)(2,1)S(1)}) custom-call(s32[8]{0:T(128)S(1)} %copy-done.2, f32[8]{0:T(128)S(1)} %copy-done.3, bf16[8,2,2,2,16,256]{5,4,3,2,1,0:T(8,128)(2,1)S(1)} %bitcast.10), custom_call_target="tpu_custom_call" | custom-call | tf_op jit(solution)/shard_map/pallas_call | solution.py:244
  70.7 4.0 %collective-permute-start.7 = (bf16[2,16,512]{2,1,0:T(8,128)(2,1)S(1)}, bf16[2,16,512]{2,1,0:T(8,128)(2,1)S(1)}, u32[]{:S(2)}, u32[]{:S(2)}) collective-permute-start(bf16[2,16,512]{2,1,0:T(8,128)(2,1)S(1)} %get-tuple-element.29), channel_id=1, source_target_pairs={{448,0},{480,32},{0,64},{32,96},{64,128},{96,160},{128,192},{160,2... | collective-permute-start | bytes 98312 | tf_op jit(solution)/shard_map/ppermute | solution.py:266
  74.8 8.6 %collective-permute-start.6 = (bf16[2,16,512]{2,1,0:T(8,128)(2,1)S(1)}, bf16[2,16,512]{2,1,0:T(8,128)(2,1)S(1)}, u32[]{:S(2)}, u32[]{:S(2)}) collective-permute-start(bf16[2,16,512]{2,1,0:T(8,128)(2,1)S(1)} %get-tuple-element.29), channel_id=1, source_target_pairs={{64,0},{96,32},{128,64},{160,96},{192,128},{224,160},{256,192},{28... | collective-permute-start | bytes 98312 | tf_op jit(solution)/shard_map/ppermute | solution.py:266
  83.4 5.7 %shard_map.97 = (bf16[2,2,256,256]{3,2,1,0:T(8,128)(2,1)S(1)}, bf16[2,2,256,256]{3,2,1,0:T(8,128)(2,1)S(1)}) custom-call(bf16[1024,1024]{1,0:T(8,128)(2,1)} %get-tuple-element.30.forward_in, bf16[1024,1024]{1,0:T(8,128)(2,1)} %get-tuple-element.31.backward_in, bf16[2,1024,256]{2,1,0:T(8,128)(2,1)} %get-tuple-element.32.green_in, ...), custom_call_target="tpu_custom_call" | custom-call | tf_op jit(solution)/shard_map/pallas_call | solution.py:244
  89.1 1.3 %collective-permute-start.11 = (bf16[2,2,256,256]{3,2,1,0:T(8,128)(2,1)S(1)}, bf16[2,2,256,256]{3,2,1,0:T(8,128)(2,1)S(1)}, u32[]{:S(2)}, u32[]{:S(2)}) collective-permute-start(bf16[2,2,256,256]{3,2,1,0:T(8,128)(2,1)S(1)} %get-tuple-element.35), channel_id=1, source_target_pairs={{0,1},{2,3},{4,5},{6,7},{8,9},{10,11},{12,13},{14,15},{16,17},{18,... | collective-permute-start | bytes 1572872 | tf_op jit(solution)/shard_map/ppermute | solution.py:358
  90.4 0.0 collective-permute-done.6
  90.5 3.3 %collective-permute-start.8 = (bf16[2,16,512]{2,1,0:T(8,128)(2,1)S(1)}, bf16[2,16,512]{2,1,0:T(8,128)(2,1)S(1)}, u32[]{:S(2)}, u32[]{:S(2)}) collective-permute-start(bf16[2,16,512]{2,1,0:T(8,128)(2,1)S(1)} %get-tuple-element.44), channel_id=1, source_target_pairs={{192,0},{224,32},{256,64},{288,96},{320,128},{352,160},{384,192},{... | collective-permute-start | bytes 98312 | tf_op jit(solution)/shard_map/ppermute | solution.py:266
  93.8 3.8 %collective-permute-start.9 = (bf16[2,16,512]{2,1,0:T(8,128)(2,1)S(1)}, bf16[2,16,512]{2,1,0:T(8,128)(2,1)S(1)}, u32[]{:S(2)}, u32[]{:S(2)}) collective-permute-start(bf16[2,16,512]{2,1,0:T(8,128)(2,1)S(1)} %get-tuple-element.45), channel_id=1, source_target_pairs={{320,0},{352,32},{384,64},{416,96},{448,128},{480,160},{0,192},{32... | collective-permute-start | bytes 98312 | tf_op jit(solution)/shard_map/ppermute | solution.py:266
  97.6 4.3 %collective-permute-done.9 = bf16[2,16,512]{2,1,0:T(8,128)(2,1)S(1)} collective-permute-done((bf16[2,16,512]{2,1,0:T(8,128)(2,1)S(1)}, bf16[2,16,512]{2,1,0:T(8,128)(2,1)S(1)}, u32[]{:S(2)}, u32[]{:S(2)}) %collective-permute-start.9) | collective-permute-done | bytes 32800 | tf_op jit(solution)/shard_map/ppermute | solution.py:266
  101.9 8.1 %collective-permute-start.10 = (bf16[2,16,512]{2,1,0:T(8,128)(2,1)S(1)}, bf16[2,16,512]{2,1,0:T(8,128)(2,1)S(1)}, u32[]{:S(2)}, u32[]{:S(2)}) collective-permute-start(bf16[2,16,512]{2,1,0:T(8,128)(2,1)S(1)} %fusion.2), channel_id=1, source_target_pairs={{0,32},{32,0},{64,96},{96,64},{128,160},{160,128},{192,224},{224,1... | collective-permute-start | bytes 98312 | tf_op jit(solution)/shard_map/ppermute | solution.py:373
  110.0 0.0 collective-permute-done.11.given_ref
  110.1 0.9 shard_map.98
  110.9 0.7 add_bitcast_fusion
  (13 shorter events, 0.1 us)
Async XLA Ops:
  0.6 17.4 %copy-start = (bf16[48,2,16,512]{3,2,1,0:T(8,128)(2,1)S(1)}, bf16[48,2,16,512]{3,2,1,0:T(8,128)(2,1)}, u32[]{:S(2)}) copy-start(bf16[48,2,16,512]{3,2,1,0:T(8,128)(2,1)} %states_ref.1) | copy-start | bytes 4718596
  0.6 17.4 %copy-start.4 = (s32[48]{0:T(128)S(1)}, s32[48]{0:T(128)}, u32[]{:S(2)}) copy-start(s32[48]{0:T(128)} %row_ref.1) | copy-start | bytes 580
  2.0 14.6 %collective-permute-start.2 = (bf16[2,2,256,256]{3,2,1,0:T(8,128)(2,1)S(1)}, bf16[2,2,256,256]{3,2,1,0:T(8,128)(2,1)S(1)}, u32[]{:S(2)}, u32[]{:S(2)}) collective-permute-start(bf16[2,2,256,256]{3,2,1,0:T(8,128)(2,1)S(1)} %get-tuple-element.43.own_ref), channel_id=1, source_target_pairs={{2,0},{0,2},{6,4},{4,6},{10,8},{8,10},{14,12},{12,14},{18,16},{16,... | collective-permute-start | bytes 1572872 | tf_op jit(solution)/shard_map/ppermute | solution.py:299
  2.7 22.1 %collective-permute-start.1 = (bf16[2,2,256,256]{3,2,1,0:T(8,128)(2,1)S(1)}, bf16[2,2,256,256]{3,2,1,0:T(8,128)(2,1)S(1)}, u32[]{:S(2)}, u32[]{:S(2)}) collective-permute-start(bf16[2,2,256,256]{3,2,1,0:T(8,128)(2,1)S(1)} %get-tuple-element.43.own_ref), channel_id=1, source_target_pairs={{3,0},{1,2},{7,4},{5,6},{11,8},{9,10},{15,12},{13,14},{19,16},{17,... | collective-permute-start | bytes 1572872 | tf_op jit(solution)/shard_map/ppermute | solution.py:299
  10.3 14.6 %collective-permute-start = (bf16[2,2,256,256]{3,2,1,0:T(8,128)(2,1)S(1)}, bf16[2,2,256,256]{3,2,1,0:T(8,128)(2,1)S(1)}, u32[]{:S(2)}, u32[]{:S(2)}) collective-permute-start(bf16[2,2,256,256]{3,2,1,0:T(8,128)(2,1)S(1)} %get-tuple-element.43.own_ref), channel_id=1, source_target_pairs={{1,0},{3,2},{5,4},{7,6},{9,8},{11,10},{13,12},{15,14},{17,16},{19,... | collective-permute-start | bytes 1572872 | tf_op jit(solution)/shard_map/ppermute | solution.py:299
  11.7 23.5 %collective-permute-start.5 = (bf16[2,2,256,256]{3,2,1,0:T(8,128)(2,1)S(1)}, bf16[2,2,256,256]{3,2,1,0:T(8,128)(2,1)S(1)}, u32[]{:S(2)}, u32[]{:S(2)}) collective-permute-start(bf16[2,2,256,256]{3,2,1,0:T(8,128)(2,1)S(1)} %get-tuple-element.42.own_ref), channel_id=1, source_target_pairs={{2,0},{0,2},{6,4},{4,6},{10,8},{8,10},{14,12},{12,14},{18,16},{16,... | collective-permute-start | bytes 1572872 | tf_op jit(solution)/shard_map/ppermute | solution.py:299
  12.4 22.8 %collective-permute-start.4 = (bf16[2,2,256,256]{3,2,1,0:T(8,128)(2,1)S(1)}, bf16[2,2,256,256]{3,2,1,0:T(8,128)(2,1)S(1)}, u32[]{:S(2)}, u32[]{:S(2)}) collective-permute-start(bf16[2,2,256,256]{3,2,1,0:T(8,128)(2,1)S(1)} %get-tuple-element.42.own_ref), channel_id=1, source_target_pairs={{3,0},{1,2},{7,4},{5,6},{11,8},{9,10},{15,12},{13,14},{19,16},{17,... | collective-permute-start | bytes 1572872 | tf_op jit(solution)/shard_map/ppermute | solution.py:299
  16.7 18.4 %collective-permute-start.3 = (bf16[2,2,256,256]{3,2,1,0:T(8,128)(2,1)S(1)}, bf16[2,2,256,256]{3,2,1,0:T(8,128)(2,1)S(1)}, u32[]{:S(2)}, u32[]{:S(2)}) collective-permute-start(bf16[2,2,256,256]{3,2,1,0:T(8,128)(2,1)S(1)} %get-tuple-element.42.own_ref), channel_id=1, source_target_pairs={{1,0},{3,2},{5,4},{7,6},{9,8},{11,10},{13,12},{15,14},{17,16},{19,... | collective-permute-start | bytes 1572872 | tf_op jit(solution)/shard_map/ppermute | solution.py:299
  18.0 1.2 %copy-start.1 = (bf16[2,512,512]{2,1,0:T(8,128)(2,1)S(1)}, bf16[2,512,512]{2,1,0:T(8,128)(2,1)}, u32[]{:S(2)}) copy-start(bf16[2,512,512]{2,1,0:T(8,128)(2,1)} %coupling_ref.1) | copy-start | bytes 3145732
  35.1 34.2 %copy-start.2 = (s32[8]{0:T(128)S(1)}, s32[8]{0:T(128)}, u32[]{:S(2)}) copy-start(s32[8]{0:T(128)} %assignment_ref.1) | copy-start | bytes 100
  35.2 34.2 %copy-start.3 = (f32[8]{0:T(128)S(1)}, f32[8]{0:T(128)}, u32[]{:S(2)}) copy-start(f32[8]{0:T(128)} %weight_ref.1) | copy-start | bytes 100
  70.7 19.7 %collective-permute-start.7 = (bf16[2,16,512]{2,1,0:T(8,128)(2,1)S(1)}, bf16[2,16,512]{2,1,0:T(8,128)(2,1)S(1)}, u32[]{:S(2)}, u32[]{:S(2)}) collective-permute-start(bf16[2,16,512]{2,1,0:T(8,128)(2,1)S(1)} %get-tuple-element.29), channel_id=1, source_target_pairs={{448,0},{480,32},{0,64},{32,96},{64,128},{96,160},{128,192},{160,2... | collective-permute-start | bytes 98312 | tf_op jit(solution)/shard_map/ppermute | solution.py:266
  74.8 15.7 %collective-permute-start.6 = (bf16[2,16,512]{2,1,0:T(8,128)(2,1)S(1)}, bf16[2,16,512]{2,1,0:T(8,128)(2,1)S(1)}, u32[]{:S(2)}, u32[]{:S(2)}) collective-permute-start(bf16[2,16,512]{2,1,0:T(8,128)(2,1)S(1)} %get-tuple-element.29), channel_id=1, source_target_pairs={{64,0},{96,32},{128,64},{160,96},{192,128},{224,160},{256,192},{28... | collective-permute-start | bytes 98312 | tf_op jit(solution)/shard_map/ppermute | solution.py:266
  89.1 20.9 %collective-permute-start.11 = (bf16[2,2,256,256]{3,2,1,0:T(8,128)(2,1)S(1)}, bf16[2,2,256,256]{3,2,1,0:T(8,128)(2,1)S(1)}, u32[]{:S(2)}, u32[]{:S(2)}) collective-permute-start(bf16[2,2,256,256]{3,2,1,0:T(8,128)(2,1)S(1)} %get-tuple-element.35), channel_id=1, source_target_pairs={{0,1},{2,3},{4,5},{6,7},{8,9},{10,11},{12,13},{14,15},{16,17},{18,... | collective-permute-start | bytes 1572872 | tf_op jit(solution)/shard_map/ppermute | solution.py:358
  90.5 7.1 %collective-permute-start.8 = (bf16[2,16,512]{2,1,0:T(8,128)(2,1)S(1)}, bf16[2,16,512]{2,1,0:T(8,128)(2,1)S(1)}, u32[]{:S(2)}, u32[]{:S(2)}) collective-permute-start(bf16[2,16,512]{2,1,0:T(8,128)(2,1)S(1)} %get-tuple-element.44), channel_id=1, source_target_pairs={{192,0},{224,32},{256,64},{288,96},{320,128},{352,160},{384,192},{... | collective-permute-start | bytes 98312 | tf_op jit(solution)/shard_map/ppermute | solution.py:266
  93.8 8.1 %collective-permute-start.9 = (bf16[2,16,512]{2,1,0:T(8,128)(2,1)S(1)}, bf16[2,16,512]{2,1,0:T(8,128)(2,1)S(1)}, u32[]{:S(2)}, u32[]{:S(2)}) collective-permute-start(bf16[2,16,512]{2,1,0:T(8,128)(2,1)S(1)} %get-tuple-element.45), channel_id=1, source_target_pairs={{320,0},{352,32},{384,64},{416,96},{448,128},{480,160},{0,192},{32... | collective-permute-start | bytes 98312 | tf_op jit(solution)/shard_map/ppermute | solution.py:266
  101.9 9.0 %collective-permute-start.10 = (bf16[2,16,512]{2,1,0:T(8,128)(2,1)S(1)}, bf16[2,16,512]{2,1,0:T(8,128)(2,1)S(1)}, u32[]{:S(2)}, u32[]{:S(2)}) collective-permute-start(bf16[2,16,512]{2,1,0:T(8,128)(2,1)S(1)} %fusion.2), channel_id=1, source_target_pairs={{0,32},{32,0},{64,96},{96,64},{128,160},{160,128},{192,224},{224,1... | collective-permute-start | bytes 98312 | tf_op jit(solution)/shard_map/ppermute | solution.py:373

commit v4 on v2

--- a/solution.py
+++ b/solution.py
@@ -255,6 +255,25 @@
     return run
 
 
+def over_energies(energies_axis, copies):
+    chips = energies_axis // 2
+    alike = [[2 * chip + core for chip in range(chips)] for core in range(2)]
+    couples = [[2 * chip, 2 * chip + 1] for chip in range(chips)]
+    gathered = lax.all_to_all(
+        copies, "energy", split_axis=0, concat_axis=0, axis_index_groups=alike, tiled=True
+    )
+    own = jnp.sum(gathered.astype(jnp.float32), axis=0).astype(copies.dtype)
+    both = lax.all_to_all(
+        jnp.stack([own, own]),
+        "energy",
+        split_axis=0,
+        concat_axis=0,
+        axis_index_groups=couples,
+        tiled=True,
+    )
+    return jnp.sum(both.astype(jnp.float32), axis=0)
+
+
 def local(energies_axis, rows_axis, coupling, inverses, contact_row, assignment, states, weights):
     half = inverses.shape[-1]
     order = 2 * half
@@ -341,25 +360,16 @@
     far_forward, far_backward = call(choose, (block_shape, block_shape), [])(kept, given)
 
     groups = assignment.shape[0]
-    chips = energies_axis // 2
     injection, weighted = call(
         spread,
         (
             jax.ShapeDtypeStruct((groups, 2, count, order), f32),
-            jax.ShapeDtypeStruct((chips, 2, count, order), bf16),
+            jax.ShapeDtypeStruct((energies_axis // 2, 2, count, order), bf16),
         ),
         [],
         scalars=2,
     )(assignment, weights, received.reshape(slots, 2, 2, 2, count, half))
-    alike = [[2 * chip + core for chip in range(chips)] for core in range(2)]
-    gathered = lax.all_to_all(
-        weighted, "energy", split_axis=0, concat_axis=0, axis_index_groups=alike, tiled=True
-    )
-    part_sum = jnp.sum(gathered.astype(f32), axis=0)
-    other_sum = lax.ppermute(
-        part_sum.astype(bf16), "energy", [(i, i ^ 1) for i in range(energies_axis)]
-    )
-    integrated = part_sum + other_sum.astype(f32)
+    integrated = over_energies(energies_axis, weighted)
     return injection[:, None], integrated[None], far_forward, far_backward
 
 

time: 101 us -> 101 us (level)
  the two profiles are of different devices: /device:TPU:2 before, /device:TPU:1 now
where the time goes in v4:
time: 101 us
  starting transfers between devices  37.3 us (37%)
  Pallas kernels  30.6 us (30%)
  waiting for transfers between devices  21.1 us (21%)
  blocking collectives  7.48 us (7%)
  local copies, waits for them, and re-layouts  2.63 us (3%)
    pallas_call x6, Pallas kernels, run(): pl.pallas_call(body, out_shape=outs, in_specs=specs, out_specs=tuple((HBM...  30.6 us
    ppermute x6, starting transfers between devices, local(): fetched[c].append(lax.ppermute(chunk, both, routes(flip, True)))  15.9 us
    all_to_all x1, starting transfers between devices, over_energies(): lax.all_to_all(copies, 'energy', split_axis=0, concat_axis=0, axis_index_...  10.1 us
    all_to_all x1, starting transfers between devices, local(): lax.all_to_all(injected, 'rows', split_axis=0, concat_axis=0, tiled=True)  10 us
    all_to_all x1, waiting for transfers between devices, local(): lax.all_to_all(injected, 'rows', split_axis=0, concat_axis=0, tiled=True)  8.9 us
    all_to_all x1, waiting for transfers between devices, over_energies(): lax.all_to_all(copies, 'energy', split_axis=0, concat_axis=0, axis_index_...  8.51 us
    all_to_all x1, blocking collectives, over_energies(): lax.all_to_all(jnp.stack([own, own]), 'energy', split_axis=0, concat_axis...  7.48 us
    ppermute x6, waiting for transfers between devices, local(): fetched[c].append(lax.ppermute(chunk, both, routes(flip, True)))  3.69 us
  transfers between devices with their start and end apart: 9, of which 3 were waited for; matrix products, arithmetic and copies ran while one was open for 0% of the time, Pallas kernels for 20%

profile of v4, /device:TPU:1, one launch (start us, length us, event | category | flops | bytes accessed | tf_op | source)
XLA Modules:
  0.0 100.6 jit_solution(6612397046701718208)
XLA Ops:
  0.7 1.4 %slice_bitcast_fusion = (bf16[2,2,256,256]{3,2,1,0:T(8,128)(2,1)S(1)}, bf16[2,2,256,256]{3,2,1,0:T(8,128)(2,1)S(1)}) fusion(bf16[1,4,2,256,256]{4,3,2,1,0:T(8,128)(2,1)} %param.7), kind=kLoop, calls=%fused_computation | loop fusion | bytes 2097152 | tf_op jit(solution)/shard_map/squeeze | solution.py:294
  2.0 0.7 collective-permute-start.2
  2.7 7.6 %collective-permute-start.1 = (bf16[2,2,256,256]{3,2,1,0:T(8,128)(2,1)S(1)}, bf16[2,2,256,256]{3,2,1,0:T(8,128)(2,1)S(1)}, u32[]{:S(2)}, u32[]{:S(2)}) collective-permute-start(bf16[2,2,256,256]{3,2,1,0:T(8,128)(2,1)S(1)} %get-tuple-element.47.own_ref), channel_id=1, source_target_pairs={{3,0},{1,2},{7,4},{5,6},{11,8},{9,10},{15,12},{13,14},{19,16},{17,... | collective-permute-start | bytes 1572872 | tf_op jit(solution)/shard_map/ppermute | solution.py:299
  10.3 1.3 %collective-permute-start = (bf16[2,2,256,256]{3,2,1,0:T(8,128)(2,1)S(1)}, bf16[2,2,256,256]{3,2,1,0:T(8,128)(2,1)S(1)}, u32[]{:S(2)}, u32[]{:S(2)}) collective-permute-start(bf16[2,2,256,256]{3,2,1,0:T(8,128)(2,1)S(1)} %get-tuple-element.47.own_ref), channel_id=1, source_target_pairs={{1,0},{3,2},{5,4},{7,6},{9,8},{11,10},{13,12},{15,14},{17,16},{19,... | collective-permute-start | bytes 1572872 | tf_op jit(solution)/shard_map/ppermute | solution.py:299
  11.7 0.7 collective-permute-start.5
  12.4 4.3 %collective-permute-start.4 = (bf16[2,2,256,256]{3,2,1,0:T(8,128)(2,1)S(1)}, bf16[2,2,256,256]{3,2,1,0:T(8,128)(2,1)S(1)}, u32[]{:S(2)}, u32[]{:S(2)}) collective-permute-start(bf16[2,2,256,256]{3,2,1,0:T(8,128)(2,1)S(1)} %get-tuple-element.46.own_ref), channel_id=1, source_target_pairs={{3,0},{1,2},{7,4},{5,6},{11,8},{9,10},{15,12},{13,14},{19,16},{17,... | collective-permute-start | bytes 1572872 | tf_op jit(solution)/shard_map/ppermute | solution.py:299
  16.7 0.0 collective-permute-done.2.down_ref
  16.7 1.3 %collective-permute-start.3 = (bf16[2,2,256,256]{3,2,1,0:T(8,128)(2,1)S(1)}, bf16[2,2,256,256]{3,2,1,0:T(8,128)(2,1)S(1)}, u32[]{:S(2)}, u32[]{:S(2)}) collective-permute-start(bf16[2,2,256,256]{3,2,1,0:T(8,128)(2,1)S(1)} %get-tuple-element.46.own_ref), channel_id=1, source_target_pairs={{1,0},{3,2},{5,4},{7,6},{9,8},{11,10},{13,12},{15,14},{17,16},{19,... | collective-permute-start | bytes 1572872 | tf_op jit(solution)/shard_map/ppermute | solution.py:299
  18.0 0.0 copy-done
  18.0 0.0 copy-start.1
  18.1 1.2 %copy-done.1 = bf16[2,512,512]{2,1,0:T(8,128)(2,1)S(1)} copy-done((bf16[2,512,512]{2,1,0:T(8,128)(2,1)S(1)}, bf16[2,512,512]{2,1,0:T(8,128)(2,1)}, u32[]{:S(2)}) %copy-start.1) | copy-done | bytes 1048600
  19.3 1.9 %shard_map.93 = (bf16[1024,1024]{1,0:T(8,128)(2,1)S(1)}, bf16[1024,1024]{1,0:T(8,128)(2,1)S(1)}, bf16[1024,1024]{1,0:T(8,128)(2,1)S(1)}) custom-call(s32[48]{0:T(128)S(1)} %copy-done.4, bf16[2,512,512]{2,1,0:T(8,128)(2,1)S(1)} %copy-done.1, bf16[48,2,16,512]{3,2,1,0:T(8,128)(2,1)S(1)} %copy-done), custom_call_target="tpu_custom_call" | custom-call | tf_op jit(solution)/shard_map/pallas_call | solution.py:246
  21.2 3.7 %collective-permute-done.1.cross_ref = bf16[2,2,256,256]{3,2,1,0:T(8,128)(2,1)S(1)} collective-permute-done((bf16[2,2,256,256]{3,2,1,0:T(8,128)(2,1)S(1)}, bf16[2,2,256,256]{3,2,1,0:T(8,128)(2,1)S(1)}, u32[]{:S(2)}, u32[]{:S(2)}) %collective-permute-start.1) | collective-permute-done | bytes 524320 | tf_op jit(solution)/shard_map/ppermute | solution.py:299
  24.9 0.0 collective-permute-done.side_ref
  24.9 10.2 %shard_map.94 = (bf16[1024,1024]{1,0:T(8,128)(2,1)S(1)}, bf16[1024,1024]{1,0:T(8,128)(2,1)S(1)}, f32[512,512]{1,0:T(8,128)S(1)}) custom-call(bf16[1024,1024]{1,0:T(8,128)(2,1)S(1)} %get-tuple-element.21.forward_in, bf16[1024,1024]{1,0:T(8,128)(2,1)S(1)} %get-tuple-element.22.backward_in, bf16[2,2,256,256]{3,2,1,0:T(8,128)(2,1)S(1)} %get-tuple-element.47.own_ref, ...), custom_call_target="tpu_custom_call" | custom-call | tf_op jit(solution)/shard_map/pallas_call | solution.py:246
  35.1 0.0 collective-permute-done.5.down_ref
  35.1 0.0 collective-permute-done.4.cross_ref
  35.1 0.0 collective-permute-done.3.side_ref
  35.1 10.4 %shard_map.95 = (bf16[1024,1024]{1,0:T(8,128)(2,1)}, bf16[1024,1024]{1,0:T(8,128)(2,1)}, bf16[2,1024,256]{2,1,0:T(8,128)(2,1)}, bf16[512,1024]{1,0:T(8,128)(2,1)}, bf16[32,2,16,256]{3,2,1,0:T(8,128)(2,1)}) custom-call(bf16[1024,1024]{1,0:T(8,128)(2,1)S(1)} %get-tuple-element.23.forward_in, bf16[1024,1024]{1,0:T(8,128)(2,1)S(1)} %get-tuple-element.24.backward_in, ...), custom_call_target="tpu_custom_call" | custom-call | tf_op jit(solution)/shard_map/pallas_call | solution.py:246
  45.5 10.0 %all-to-all-start = ((bf16[32,2,16,256]{3,2,1,0:T(8,128)(2,1)}), bf16[32,2,16,256]{3,2,1,0:T(8,128)(2,1)S(1)}, u32[]{:S(2)}, u32[]{:S(2)}) async-start(bf16[32,2,16,256]{3,2,1,0:T(8,128)(2,1)} %get-tuple-element.27), calls=%async_computation | async-start | bytes 1048576 | tf_op jit(solution)/shard_map/all_to_all | solution.py:342
  55.5 0.0 copy-start.2
  55.6 0.0 copy-start.3
  55.6 5.7 %shard_map.97 = (bf16[2,2,256,256]{3,2,1,0:T(8,128)(2,1)S(1)}, bf16[2,2,256,256]{3,2,1,0:T(8,128)(2,1)S(1)}) custom-call(bf16[1024,1024]{1,0:T(8,128)(2,1)} %get-tuple-element.30.forward_in, bf16[1024,1024]{1,0:T(8,128)(2,1)} %get-tuple-element.31.backward_in, bf16[2,1024,256]{2,1,0:T(8,128)(2,1)} %get-tuple-element.32.green_in, ...), custom_call_target="tpu_custom_call" | custom-call | tf_op jit(solution)/shard_map/pallas_call | solution.py:246
  61.3 1.3 %collective-permute-start.6 = (bf16[2,2,256,256]{3,2,1,0:T(8,128)(2,1)S(1)}, bf16[2,2,256,256]{3,2,1,0:T(8,128)(2,1)S(1)}, u32[]{:S(2)}, u32[]{:S(2)}) collective-permute-start(bf16[2,2,256,256]{3,2,1,0:T(8,128)(2,1)S(1)} %get-tuple-element.35), channel_id=1, source_target_pairs={{0,1},{2,3},{4,5},{6,7},{8,9},{10,11},{12,13},{14,15},{16,17},{18,... | collective-permute-start | bytes 1572872 | tf_op jit(solution)/shard_map/ppermute | solution.py:358
  62.6 8.9 %all-to-all-done = bf16[32,2,16,256]{3,2,1,0:T(8,128)(2,1)S(1)} async-done(((bf16[32,2,16,256]{3,2,1,0:T(8,128)(2,1)}), bf16[32,2,16,256]{3,2,1,0:T(8,128)(2,1)S(1)}, u32[]{:S(2)}, u32[]{:S(2)}) %all-to-all-start) | async-done | bytes 524320 | tf_op jit(solution)/shard_map/all_to_all | solution.py:342
  71.5 1.5 %shard_map.96 = (f32[8,2,16,512]{3,2,1,0:T(8,128)}, bf16[8,2,16,512]{3,2,1,0:T(8,128)(2,1)}) custom-call(s32[8]{0:T(128)S(1)} %copy-done.2, f32[8]{0:T(128)S(1)} %copy-done.3, bf16[8,2,2,2,16,256]{5,4,3,2,1,0:T(8,128)(2,1)S(1)} %bitcast.10), custom_call_target="tpu_custom_call" | custom-call | tf_op jit(solution)/shard_map/pallas_call | solution.py:246
  73.0 10.1 %all-to-all-start.1 = ((bf16[8,2,16,512]{3,2,1,0:T(8,128)(2,1)}), bf16[8,2,16,512]{3,2,1,0:T(8,128)(2,1)S(1)}, u32[]{:S(2)}, u32[]{:S(2)}) async-start(bf16[8,2,16,512]{3,2,1,0:T(8,128)(2,1)} %get-tuple-element.29), calls=%async_computation.1 | async-start | bytes 524288 | tf_op jit(solution)/shard_map/all_to_all | solution.py:262
  83.1 0.0 collective-permute-done.6.given_ref
  83.1 0.9 shard_map.98
  83.9 8.5 %all-to-all-done.1 = bf16[8,2,16,512]{3,2,1,0:T(8,128)(2,1)S(1)} async-done(((bf16[8,2,16,512]{3,2,1,0:T(8,128)(2,1)}), bf16[8,2,16,512]{3,2,1,0:T(8,128)(2,1)S(1)}, u32[]{:S(2)}, u32[]{:S(2)}) %all-to-all-start.1) | async-done | bytes 262176 | tf_op jit(solution)/shard_map/all_to_all | solution.py:262
  92.5 7.5 %all_to_all.15 = bf16[2,2,16,512]{3,2,1,0:T(8,128)(2,1)S(1)} all-to-all(bf16[2,2,16,512]{3,2,1,0:T(8,128)(2,1)S(1)} %pad_maximum_fusion), channel_id=1, replica_groups={{0,32},{64,96},{128,160},{192,224},{256,288},{320,352},{384,416},{448,4..., dimensions={0} | all-to-all | bytes 131072 | tf_op jit(solution)/shard_map/all_to_all | solution.py:266
  100.0 0.6 convert_reduce_fusion
  (7 shorter events, 0.1 us)
Async XLA Ops:
  0.6 17.4 %copy-start = (bf16[48,2,16,512]{3,2,1,0:T(8,128)(2,1)S(1)}, bf16[48,2,16,512]{3,2,1,0:T(8,128)(2,1)}, u32[]{:S(2)}) copy-start(bf16[48,2,16,512]{3,2,1,0:T(8,128)(2,1)} %states_ref.1) | copy-start | bytes 4718596
  0.6 17.4 %copy-start.4 = (s32[48]{0:T(128)S(1)}, s32[48]{0:T(128)}, u32[]{:S(2)}) copy-start(s32[48]{0:T(128)} %row_ref.1) | copy-start | bytes 580
  2.0 14.6 %collective-permute-start.2 = (bf16[2,2,256,256]{3,2,1,0:T(8,128)(2,1)S(1)}, bf16[2,2,256,256]{3,2,1,0:T(8,128)(2,1)S(1)}, u32[]{:S(2)}, u32[]{:S(2)}) collective-permute-start(bf16[2,2,256,256]{3,2,1,0:T(8,128)(2,1)S(1)} %get-tuple-element.47.own_ref), channel_id=1, source_target_pairs={{2,0},{0,2},{6,4},{4,6},{10,8},{8,10},{14,12},{12,14},{18,16},{16,... | collective-permute-start | bytes 1572872 | tf_op jit(solution)/shard_map/ppermute | solution.py:299
  2.7 22.1 %collective-permute-start.1 = (bf16[2,2,256,256]{3,2,1,0:T(8,128)(2,1)S(1)}, bf16[2,2,256,256]{3,2,1,0:T(8,128)(2,1)S(1)}, u32[]{:S(2)}, u32[]{:S(2)}) collective-permute-start(bf16[2,2,256,256]{3,2,1,0:T(8,128)(2,1)S(1)} %get-tuple-element.47.own_ref), channel_id=1, source_target_pairs={{3,0},{1,2},{7,4},{5,6},{11,8},{9,10},{15,12},{13,14},{19,16},{17,... | collective-permute-start | bytes 1572872 | tf_op jit(solution)/shard_map/ppermute | solution.py:299
  10.3 14.6 %collective-permute-start = (bf16[2,2,256,256]{3,2,1,0:T(8,128)(2,1)S(1)}, bf16[2,2,256,256]{3,2,1,0:T(8,128)(2,1)S(1)}, u32[]{:S(2)}, u32[]{:S(2)}) collective-permute-start(bf16[2,2,256,256]{3,2,1,0:T(8,128)(2,1)S(1)} %get-tuple-element.47.own_ref), channel_id=1, source_target_pairs={{1,0},{3,2},{5,4},{7,6},{9,8},{11,10},{13,12},{15,14},{17,16},{19,... | collective-permute-start | bytes 1572872 | tf_op jit(solution)/shard_map/ppermute | solution.py:299
  11.7 23.5 %collective-permute-start.5 = (bf16[2,2,256,256]{3,2,1,0:T(8,128)(2,1)S(1)}, bf16[2,2,256,256]{3,2,1,0:T(8,128)(2,1)S(1)}, u32[]{:S(2)}, u32[]{:S(2)}) collective-permute-start(bf16[2,2,256,256]{3,2,1,0:T(8,128)(2,1)S(1)} %get-tuple-element.46.own_ref), channel_id=1, source_target_pairs={{2,0},{0,2},{6,4},{4,6},{10,8},{8,10},{14,12},{12,14},{18,16},{16,... | collective-permute-start | bytes 1572872 | tf_op jit(solution)/shard_map/ppermute | solution.py:299
  12.4 22.8 %collective-permute-start.4 = (bf16[2,2,256,256]{3,2,1,0:T(8,128)(2,1)S(1)}, bf16[2,2,256,256]{3,2,1,0:T(8,128)(2,1)S(1)}, u32[]{:S(2)}, u32[]{:S(2)}) collective-permute-start(bf16[2,2,256,256]{3,2,1,0:T(8,128)(2,1)S(1)} %get-tuple-element.46.own_ref), channel_id=1, source_target_pairs={{3,0},{1,2},{7,4},{5,6},{11,8},{9,10},{15,12},{13,14},{19,16},{17,... | collective-permute-start | bytes 1572872 | tf_op jit(solution)/shard_map/ppermute | solution.py:299
  16.7 18.4 %collective-permute-start.3 = (bf16[2,2,256,256]{3,2,1,0:T(8,128)(2,1)S(1)}, bf16[2,2,256,256]{3,2,1,0:T(8,128)(2,1)S(1)}, u32[]{:S(2)}, u32[]{:S(2)}) collective-permute-start(bf16[2,2,256,256]{3,2,1,0:T(8,128)(2,1)S(1)} %get-tuple-element.46.own_ref), channel_id=1, source_target_pairs={{1,0},{3,2},{5,4},{7,6},{9,8},{11,10},{13,12},{15,14},{17,16},{19,... | collective-permute-start | bytes 1572872 | tf_op jit(solution)/shard_map/ppermute | solution.py:299
  18.0 1.2 %copy-start.1 = (bf16[2,512,512]{2,1,0:T(8,128)(2,1)S(1)}, bf16[2,512,512]{2,1,0:T(8,128)(2,1)}, u32[]{:S(2)}) copy-start(bf16[2,512,512]{2,1,0:T(8,128)(2,1)} %coupling_ref.1) | copy-start | bytes 3145732
  45.5 26.0 %all-to-all-start = ((bf16[32,2,16,256]{3,2,1,0:T(8,128)(2,1)}), bf16[32,2,16,256]{3,2,1,0:T(8,128)(2,1)S(1)}, u32[]{:S(2)}, u32[]{:S(2)}) async-start(bf16[32,2,16,256]{3,2,1,0:T(8,128)(2,1)} %get-tuple-element.27), calls=%async_computation | async-start | bytes 1048576 | tf_op jit(solution)/shard_map/all_to_all | solution.py:342
  55.5 16.0 %copy-start.2 = (s32[8]{0:T(128)S(1)}, s32[8]{0:T(128)}, u32[]{:S(2)}) copy-start(s32[8]{0:T(128)} %assignment_ref.1) | copy-start | bytes 100
  55.6 16.0 %copy-start.3 = (f32[8]{0:T(128)S(1)}, f32[8]{0:T(128)}, u32[]{:S(2)}) copy-start(f32[8]{0:T(128)} %weight_ref.1) | copy-start | bytes 100
  61.3 21.8 %collective-permute-start.6 = (bf16[2,2,256,256]{3,2,1,0:T(8,128)(2,1)S(1)}, bf16[2,2,256,256]{3,2,1,0:T(8,128)(2,1)S(1)}, u32[]{:S(2)}, u32[]{:S(2)}) collective-permute-start(bf16[2,2,256,256]{3,2,1,0:T(8,128)(2,1)S(1)} %get-tuple-element.35), channel_id=1, source_target_pairs={{0,1},{2,3},{4,5},{6,7},{8,9},{10,11},{12,13},{14,15},{16,17},{18,... | collective-permute-start | bytes 1572872 | tf_op jit(solution)/shard_map/ppermute | solution.py:358
  73.0 19.4 %all-to-all-start.1 = ((bf16[8,2,16,512]{3,2,1,0:T(8,128)(2,1)}), bf16[8,2,16,512]{3,2,1,0:T(8,128)(2,1)S(1)}, u32[]{:S(2)}, u32[]{:S(2)}) async-start(bf16[8,2,16,512]{3,2,1,0:T(8,128)(2,1)} %get-tuple-element.29), calls=%async_computation.1 | async-start | bytes 524288 | tf_op jit(solution)/shard_map/all_to_all | solution.py:262
